TPU v7x, 32 devices: a whole 2x2x4 slice. The times are simulated.
32 devices in a mesh: face: 8 (over z, y), col: 4 (over x, core).
Axes of the slice: x: 2, y: 2, z: 4, core: 2. Of those that a mesh axis runs over, the one named last changes fastest.
Arguments:
- fields: float32 [4, 160, 80, 128], P(None, 'face', 'col'), may hold values from -6 to 6
- metric_diag: float32 [2, 160, 80], P(None, 'face', 'col'), may hold values from 0.05 to 0.5
- metric_cross: float32 [160, 80], P('face', 'col'), may hold values from -0.1 to 0.1
- point_mass: float32 [160, 80], P('face', 'col'), may hold values from 0.5 to 2
Outputs:
- biharmonic: float32 [4, 160, 80, 128], P(None, 'face', 'col')
All inputs are finite; a program needn't handle non-finite values.
Results may differ from a plain program's by a relative error of at most 0.00024.
Values sent between devices are 32-bit elements; how exact they have to be, the bound alone decides.
No kernel may reach another device: no remote copies, remote signals or barrier semaphores. Data moves between devices by JAX's collectives and lax.ppermute only.
A program may use at most 64 MiB of HBM per device.

v0:
```python
import jax
import jax.numpy as jnp
import numpy as np
from jax import lax
from jax.sharding import PartitionSpec as P


def with_halo(array, sides, width):
    for axis, dim in sides:
        devices, length = (lax.axis_size(axis), array.shape[dim])
        up = [(i, (i + 1) % devices) for i in range(devices)]
        down = [(j, i) for i, j in up]
        last = lax.slice_in_dim(array, length - width, length, axis=dim)
        first = lax.slice_in_dim(array, 0, width, axis=dim)
        before = lax.ppermute(last, axis, up)
        after = lax.ppermute(first, axis, down)
        array = jnp.concatenate([before, array, after], axis=dim)
    return array


def derivative_table():
    small = 1.0 / np.sqrt(5.0)
    nodes = np.array([-1.0, -small, small, 1.0])
    count = nodes.shape[0]
    weights = np.array(
        [np.prod([nodes[a] - nodes[k] for k in range(count) if k != a]) for a in range(count)]
    )
    table = np.zeros((count, count))
    for a in range(count):
        for b in range(count):
            if a == b:
                table[a, b] = np.sum([1.0 / (nodes[a] - nodes[k]) for k in range(count) if k != a])
            else:
                table[a, b] = weights[a] / weights[b] / (nodes[a] - nodes[b])
    return jnp.asarray(table, jnp.float32)


def laplace(values, metric_diag, metric_cross):
    table = derivative_table()
    nfield, rows, cols, nlev = values.shape
    blocks_x = rows // 4
    blocks_y = cols // 4
    shaped = values.reshape(nfield, blocks_x, 4, blocks_y, 4, nlev)
    first_diag = metric_diag[0].reshape(1, blocks_x, 4, blocks_y, 4, 1)
    second_diag = metric_diag[1].reshape(1, blocks_x, 4, blocks_y, 4, 1)
    cross_term = metric_cross.reshape(1, blocks_x, 4, blocks_y, 4, 1)
    high = lax.Precision.HIGHEST
    grad_x = jnp.einsum("ab,febgcl->feagcl", table, shaped, precision=high)
    grad_y = jnp.einsum("cd,febgdl->febgcl", table, shaped, precision=high)
    flux_x = first_diag * grad_x + cross_term * grad_y
    flux_y = cross_term * grad_x + second_diag * grad_y
    weak = jnp.einsum("ba,febgcl->feagcl", table, flux_x, precision=high)
    weak = weak + jnp.einsum("dc,febgdl->febgcl", table, flux_y, precision=high)
    return (-weak).reshape(nfield, rows, cols, nlev)


def assemble(padded):
    rows = padded.shape[1] - 2
    cols = padded.shape[2] - 2
    row_local = jnp.arange(rows, dtype=jnp.int32) % 4
    col_local = jnp.arange(cols, dtype=jnp.int32) % 4
    row_low = (row_local == 0).astype(jnp.float32).reshape(1, rows, 1, 1)
    row_high = (row_local == 3).astype(jnp.float32).reshape(1, rows, 1, 1)
    col_low = (col_local == 0).astype(jnp.float32).reshape(1, 1, cols, 1)
    col_high = (col_local == 3).astype(jnp.float32).reshape(1, 1, cols, 1)
    summed = padded[:, 1:-1] + row_low * padded[:, :-2] + row_high * padded[:, 2:]
    return summed[:, :, 1:-1] + col_low * summed[:, :, :-2] + col_high * summed[:, :, 2:]


def shards(fields, metric_diag, metric_cross, point_mass):
    local_mass = point_mass[None, :, :, None]
    first_lap = laplace(fields, metric_diag, metric_cross)
    padded_lap, padded_mass = (
        with_halo(first_lap, (("face", 1), ("col", 2)), 1),
        with_halo(local_mass, (("face", 1), ("col", 2)), 1),
    )
    mass_sum = assemble(padded_mass)
    first = assemble(padded_lap) / mass_sum
    second_lap = laplace(first, metric_diag, metric_cross)
    padded_second = with_halo(second_lap, (("face", 1), ("col", 2)), 1)
    return assemble(padded_second) / mass_sum


def solution(mesh):
    return jax.shard_map(
        shards,
        mesh=mesh,
        in_specs=(
            P(None, "face", "col", None),
            P(None, "face", "col"),
            P("face", "col"),
            P("face", "col"),
        ),
        out_specs=P(None, "face", "col", None),
        check_vma=False,
    )
```

profile of v0, /device:TPU:1, one launch (start us, length us, event | category | flops | bytes accessed | tf_op | source)
XLA Modules:
  0.0 51.2 jit_solution(9082121004730212008)
XLA Ops:
  0.0 0.8 %fusion.41 = (f32[1,1,20,1]{2,1,3,0:T(1,128)S(1)}, f32[1,1,20,1]{2,1,3,0:T(1,128)S(1)}) fusion(f32[1,20,20,1]{2,1,3,0:T(8,128)} %bitcast.70), kind=kLoop, calls=%fused_computation.78 | loop fusion | bytes 320 | tf_op jit(solution)/shard_map/slice | solution.py:13
  0.8 2.1 %collective-permute-start.4 = (f32[1,1,20,1]{2,1,3,0:T(1,128)S(1)}, f32[1,1,20,1]{2,1,3,0:T(1,128)S(1)}, u32[]{:S(2)}, u32[]{:S(2)}) collective-permute-start(f32[1,1,20,1]{2,1,3,0:T(1,128)S(1)} %get-tuple-element.17), channel_id=1, source_target_pairs={{0,4},{4,8},{8,12},{12,16},{16,20},{20,24},{24,28},{28,0},{1,5},{5... | collective-permute-start | bytes 248 | tf_op jit(solution)/shard_map/ppermute | solution.py:15
  2.8 3.0 %collective-permute-start.5 = (f32[1,1,20,1]{2,1,3,0:T(1,128)S(1)}, f32[1,1,20,1]{2,1,3,0:T(1,128)S(1)}, u32[]{:S(2)}, u32[]{:S(2)}) collective-permute-start(f32[1,1,20,1]{2,1,3,0:T(1,128)S(1)} %get-tuple-element.18), channel_id=1, source_target_pairs={{4,0},{8,4},{12,8},{16,12},{20,16},{24,20},{28,24},{0,28},{5,1},{9... | collective-permute-start | bytes 248 | tf_op jit(solution)/shard_map/ppermute | solution.py:16
  5.9 0.9 %slice_reduce_fusion.1 = (f32[20,20]{1,0:T(8,128)S(1)}, f32[20,20]{1,0:T(8,128)S(1)}) fusion(f32[2,20,20]{2,0,1:T(2,128)} %param.7), kind=kLoop, calls=%fused_computation.71 | loop fusion | bytes 6400 | tf_op jit(solution)/shard_map/slice | solution.py:44
  7.5 0.4 copy-done.3
  8.2 0.4 copy-done.1
  8.7 1.5 %fusion.21 = f32[4,4,5,4,5,128]{5,0,4,3,2,1:T(4,128)S(1)} fusion(f32[4,4,1,1,1,1]{1,0,5,4,3,2:T(4,128)S(1)} %copy-done.1, f32[4,5,4,5,4,128]{5,0,4,3,2,1:T(4,128)S(1)} %bitcast.61), kind=kOutput, calls=%fused_computation.41 | convolution fusion | flops 9830400 | bytes 1638464 | tf_op jit(solution)/shard_map/cd,febgdl->febgcl/dot_general | solution.py:49
  10.1 2.0 %bitcast_add_fusion.3 = (f32[4,5,4,5,4,128]{5,2,4,3,1,0:T(4,128)S(1)}, f32[4,5,4,5,4,128]{5,2,4,3,1,0:T(4,128)S(1)}) fusion(f32[4,4,5,4,5,128]{5,0,4,3,2,1:T(4,128)S(1)} %fusion.21, f32[5,4,5,4]{1,3,2,0:T(4,128)S(1)} %copy.33, f32[5,4,5,4]{1,3,2,0:T(4,128)S(1)} %copy.28, f32[4,4,1,1,1,1]{1,0,5,4,3,2:T(4,128)S(1)} %copy-done.1, ...), kind=kOutput, calls=%fused_computation.30 | convolution fusion | flops 10444800 | bytes 3280064 | tf_op jit(solution)/shard_map/ab,febgcl->feagcl/dot_general | solution.py:48
  12.1 1.6 %fusion.19 = f32[4,5,4,5,128,4]{4,5,3,2,1,0:T(4,128)S(1)} fusion(f32[4,4,1,1,1,1]{1,0,5,4,3,2:T(4,128)S(1)} %copy-done.1, f32[4,5,4,5,4,128]{5,2,4,3,1,0:T(4,128)S(1)} %get-tuple-element.19), kind=kOutput, calls=%fused_computation.39 | convolution fusion | flops 9830400 | bytes 1638464 | tf_op jit(solution)/shard_map/dc,febgdl->febgcl/dot_general | solution.py:53
  13.7 1.9 %fusion.1 = f32[4,5,4,5,4,128]{5,2,4,3,1,0:T(4,128)S(1)} fusion(f32[4,4,1,1,1,1]{1,0,5,4,3,2:T(4,128)S(1)} %copy-done.1, f32[4,5,4,5,128,4]{4,5,3,2,1,0:T(4,128)S(1)} %fusion.19, f32[4,5,4,5,4,128]{5,2,4,3,1,0:T(4,128)S(1)} %get-tuple-element.20, f32[4,4,5,4,5,128]{5,0,4,3,2,1:T(4,128)S(1)} %fusion.21, f32[5,4,5,4]{1,3,2,0:T(4,128)S(1)} %copy.28, ...), kind=kOutput, calls=%fused_computation.5 | convolution fusion | flops 10854400 | bytes 3280064 | tf_op jit(solution)/shard_map/ba,febgcl->feagcl/dot_general | solution.py:52
  15.6 0.3 copy.37
  16.0 4.1 %collective-permute-start.1 = (f32[4,1,20,128]{3,0,2,1:T(4,128)S(1)}, f32[4,1,20,128]{3,0,2,1:T(4,128)S(1)}, u32[]{:S(2)}, u32[]{:S(2)}) collective-permute-start(f32[4,1,20,128]{3,0,2,1:T(4,128)S(1)} %get-tuple-element.14), channel_id=1, source_target_pairs={{4,0},{8,4},{12,8},{16,12},{20,16},{24,20},{28,24},{0,28},{5,1},{9... | collective-permute-start | bytes 122888 | tf_op jit(solution)/shard_map/ppermute | solution.py:16
  20.3 2.8 %collective-permute-start.6 = (f32[1,22,1,1]{2,1,3,0:T(8,128)S(1)}, f32[1,22,1,1]{2,1,3,0:T(8,128)S(1)}, u32[]{:S(2)}, u32[]{:S(2)}) collective-permute-start(f32[1,22,1,1]{2,1,3,0:T(8,128)S(1)} %get-tuple-element.15), channel_id=1, source_target_pairs={{0,1},{1,2},{2,3},{3,0},{4,5},{5,6},{6,7},{7,4},{8,9},{9,10},{10,1... | collective-permute-start | bytes 272 | tf_op jit(solution)/shard_map/ppermute | solution.py:15
  23.1 0.8 %collective-permute-done.6 = f32[1,22,1,1]{2,1,3,0:T(8,128)S(1)} collective-permute-done((f32[1,22,1,1]{2,1,3,0:T(8,128)S(1)}, f32[1,22,1,1]{2,1,3,0:T(8,128)S(1)}, u32[]{:S(2)}, u32[]{:S(2)}) %collective-permute-start.6) | collective-permute-done | bytes 120 | tf_op jit(solution)/shard_map/ppermute | solution.py:15
  23.9 2.3 %collective-permute-done.7 = f32[1,22,1,1]{2,1,3,0:T(8,128)S(1)} collective-permute-done((f32[1,22,1,1]{2,1,3,0:T(8,128)S(1)}, f32[1,22,1,1]{2,1,3,0:T(8,128)S(1)}, u32[]{:S(2)}, u32[]{:S(2)}) %collective-permute-start.7) | collective-permute-done | bytes 120 | tf_op jit(solution)/shard_map/ppermute | solution.py:16
  26.5 0.5 collective-permute-start.3
  27.0 0.6 %collective-permute-done.2 = f32[4,22,1,128]{3,0,2,1:T(4,128)S(1)} collective-permute-done((f32[4,22,1,128]{3,0,2,1:T(4,128)S(1)}, f32[4,22,1,128]{3,0,2,1:T(4,128)S(1)}, u32[]{:S(2)}, u32[]{:S(2)}) %collective-permute-start.2) | collective-permute-done | bytes 45088 | tf_op jit(solution)/shard_map/ppermute | solution.py:15
  27.7 2.5 %collective-permute-done.3 = f32[4,22,1,128]{3,0,2,1:T(4,128)S(1)} collective-permute-done((f32[4,22,1,128]{3,0,2,1:T(4,128)S(1)}, f32[4,22,1,128]{3,0,2,1:T(4,128)S(1)}, u32[]{:S(2)}, u32[]{:S(2)}) %collective-permute-start.3) | collective-permute-done | bytes 45088 | tf_op jit(solution)/shard_map/ppermute | solution.py:16
  30.4 0.3 fusion.6
  30.7 0.7 %fusion.12 = f32[4,20,20,128]{3,0,2,1:T(4,128)S(1)} fusion(f32[4,20,22,128]{3,0,2,1:T(4,128)S(1)} %fusion.6, f32[20,20]{1,0:T(8,128)S(1)} %fusion.34, f32[20]{0:T(128)S(1)} %get-tuple-element.23, f32[20]{0:T(128)S(1)} %get-tuple-element.24), kind=kLoop, calls=%fused_computation.25 | loop fusion | flops 1024000 | bytes 3278560 | tf_op jit(solution)/shard_map/div | solution.py:78
  31.5 1.5 %fusion.16 = f32[4,5,4,5,128,4]{4,5,3,2,1,0:T(4,128)S(1)} fusion(f32[4,4,1,1,1,1]{1,0,5,4,3,2:T(4,128)S(1)} %copy-done.1, f32[4,5,4,5,4,128]{5,0,4,3,2,1:T(4,128)S(1)} %bitcast.68), kind=kOutput, calls=%fused_computation.36 | convolution fusion | flops 9830400 | bytes 1638464 | tf_op jit(solution)/shard_map/cd,febgdl->febgcl/dot_general | solution.py:49
  33.0 2.0 %bitcast_add_fusion = (f32[4,5,4,5,4,128]{5,2,4,3,1,0:T(4,128)S(1)}, f32[4,5,4,5,4,128]{5,2,4,3,1,0:T(4,128)S(1)}) fusion(f32[4,5,4,5,128,4]{4,5,3,2,1,0:T(4,128)S(1)} %fusion.16, f32[5,4,5,4]{1,3,2,0:T(4,128)S(1)} %copy.33, f32[5,4,5,4]{1,3,2,0:T(4,128)S(1)} %copy.28, f32[4,4,1,1,1,1]{1,0,5,4,3,2:T(4,128)S(1)} %copy-done.1, ...), kind=kOutput, calls=%fused_computation.28 | convolution fusion | flops 10444800 | bytes 3280064 | tf_op jit(solution)/shard_map/ab,febgcl->feagcl/dot_general | solution.py:48
  35.0 1.6 %fusion.14 = f32[4,5,4,5,128,4]{4,5,3,2,1,0:T(4,128)S(1)} fusion(f32[4,4,1,1,1,1]{1,0,5,4,3,2:T(4,128)S(1)} %copy-done.1, f32[4,5,4,5,4,128]{5,2,4,3,1,0:T(4,128)S(1)} %get-tuple-element.21), kind=kOutput, calls=%fused_computation.34 | convolution fusion | flops 9830400 | bytes 1638464 | tf_op jit(solution)/shard_map/dc,febgdl->febgcl/dot_general | solution.py:53
  36.6 1.9 %fusion.3 = f32[4,5,4,5,4,128]{5,2,4,3,1,0:T(4,128)S(1)} fusion(f32[4,4,1,1,1,1]{1,0,5,4,3,2:T(4,128)S(1)} %copy-done.1, f32[4,5,4,5,128,4]{4,5,3,2,1,0:T(4,128)S(1)} %fusion.14, f32[4,5,4,5,4,128]{5,2,4,3,1,0:T(4,128)S(1)} %get-tuple-element.22, f32[4,5,4,5,128,4]{4,5,3,2,1,0:T(4,128)S(1)} %fusion.16, f32[5,4,5,4]{1,3,2,0:T(4,128)S(1)} %copy.28, ...), kind=kOutput, calls=%fused_computation.7 | convolution fusion | flops 10854400 | bytes 3280064 | tf_op jit(solution)/shard_map/ba,febgcl->feagcl/dot_general | solution.py:52
  38.5 0.3 copy.46
  38.9 4.1 %collective-permute-start.9 = (f32[4,1,20,128]{3,0,2,1:T(4,128)S(1)}, f32[4,1,20,128]{3,0,2,1:T(4,128)S(1)}, u32[]{:S(2)}, u32[]{:S(2)}) collective-permute-start(f32[4,1,20,128]{3,0,2,1:T(4,128)S(1)} %get-tuple-element.12), channel_id=1, source_target_pairs={{4,0},{8,4},{12,8},{16,12},{20,16},{24,20},{28,24},{0,28},{5,1},{9... | collective-permute-start | bytes 122888 | tf_op jit(solution)/shard_map/ppermute | solution.py:16
  43.1 1.4 %collective-permute-done.8 = f32[4,1,20,128]{3,0,2,1:T(4,128)S(1)} collective-permute-done((f32[4,1,20,128]{3,0,2,1:T(4,128)S(1)}, f32[4,1,20,128]{3,0,2,1:T(4,128)S(1)}, u32[]{:S(2)}, u32[]{:S(2)}) %collective-permute-start.8) | collective-permute-done | bytes 40992 | tf_op jit(solution)/shard_map/ppermute | solution.py:15
  44.5 1.2 %collective-permute-start.10 = (f32[4,22,1,128]{3,0,2,1:T(4,128)S(1)}, f32[4,22,1,128]{3,0,2,1:T(4,128)S(1)}, u32[]{:S(2)}, u32[]{:S(2)}) collective-permute-start(f32[4,22,1,128]{3,0,2,1:T(4,128)S(1)} %get-tuple-element.7), channel_id=1, source_target_pairs={{0,1},{1,2},{2,3},{3,0},{4,5},{5,6},{6,7},{7,4},{8,9},{9,10},{10,1... | collective-permute-start | bytes 135176 | tf_op jit(solution)/shard_map/ppermute | solution.py:15
  45.7 1.1 %collective-permute-done.10 = f32[4,22,1,128]{3,0,2,1:T(4,128)S(1)} collective-permute-done((f32[4,22,1,128]{3,0,2,1:T(4,128)S(1)}, f32[4,22,1,128]{3,0,2,1:T(4,128)S(1)}, u32[]{:S(2)}, u32[]{:S(2)}) %collective-permute-start.10) | collective-permute-done | bytes 45088 | tf_op jit(solution)/shard_map/ppermute | solution.py:15
  46.8 2.3 %collective-permute-done.11 = f32[4,22,1,128]{3,0,2,1:T(4,128)S(1)} collective-permute-done((f32[4,22,1,128]{3,0,2,1:T(4,128)S(1)}, f32[4,22,1,128]{3,0,2,1:T(4,128)S(1)}, u32[]{:S(2)}, u32[]{:S(2)}) %collective-permute-start.11) | collective-permute-done | bytes 45088 | tf_op jit(solution)/shard_map/ppermute | solution.py:16
  49.4 0.3 fusion.4
  49.7 1.5 %fusion.9 = f32[4,20,20,128]{3,0,2,1:T(4,128)} fusion(f32[4,20,22,128]{3,0,2,1:T(4,128)S(1)} %fusion.4, f32[20,20]{1,0:T(8,128)S(1)} %fusion.34, f32[20]{0:T(128)S(1)} %get-tuple-element.23, f32[20]{0:T(128)S(1)} %get-tuple-element.24), kind=kLoop, calls=%fused_computation.20 | loop fusion | flops 1024000 | bytes 3278560 | tf_op jit(solution)/shard_map/div | solution.py:81
  (34 shorter events, 2.1 us)
Async XLA Ops:
  0.0 8.2 %copy-start = (f32[4,20,20,128]{3,0,2,1:T(4,128)S(1)}, f32[4,20,20,128]{3,0,2,1:T(4,128)}, u32[]{:S(2)}) copy-start(f32[4,20,20,128]{3,0,2,1:T(4,128)} %param.6) | copy-start | bytes 2457604
  0.8 19.4 %collective-permute-start.4 = (f32[1,1,20,1]{2,1,3,0:T(1,128)S(1)}, f32[1,1,20,1]{2,1,3,0:T(1,128)S(1)}, u32[]{:S(2)}, u32[]{:S(2)}) collective-permute-start(f32[1,1,20,1]{2,1,3,0:T(1,128)S(1)} %get-tuple-element.17), channel_id=1, source_target_pairs={{0,4},{4,8},{8,12},{12,16},{16,20},{20,24},{24,28},{28,0},{1,5},{5... | collective-permute-start | bytes 248 | tf_op jit(solution)/shard_map/ppermute | solution.py:15
  2.8 17.4 %collective-permute-start.5 = (f32[1,1,20,1]{2,1,3,0:T(1,128)S(1)}, f32[1,1,20,1]{2,1,3,0:T(1,128)S(1)}, u32[]{:S(2)}, u32[]{:S(2)}) collective-permute-start(f32[1,1,20,1]{2,1,3,0:T(1,128)S(1)} %get-tuple-element.18), channel_id=1, source_target_pairs={{4,0},{8,4},{12,8},{16,12},{20,16},{24,20},{28,24},{0,28},{5,1},{9... | collective-permute-start | bytes 248 | tf_op jit(solution)/shard_map/ppermute | solution.py:16
  7.2 0.7 %copy-start.3 = (f32[20,20]{1,0:T(8,128)S(1)}, f32[20,20]{1,0:T(8,128)}, u32[]{:S(2)}) copy-start(f32[20,20]{1,0:T(8,128)} %param.8) | copy-start | bytes 4804
  8.0 0.7 %copy-start.1 = (f32[4,4,1,1,1,1]{1,0,5,4,3,2:T(4,128)S(1)}, f32[4,4,1,1,1,1]{1,0,5,4,3,2:T(4,128)}, u32[]{:S(2)}) copy-start(f32[4,4,1,1,1,1]{1,0,5,4,3,2:T(4,128)} %constant.40) | copy-start | bytes 196
  16.0 4.3 %copy-start.2 = (f32[20,20]{1,0:T(8,128)S(1)}, f32[20,20]{1,0:T(8,128)}, u32[]{:S(2)}) copy-start(f32[20,20]{1,0:T(8,128)} %param.9) | copy-start | bytes 4804
  16.0 10.4 %collective-permute-start = (f32[4,1,20,128]{3,0,2,1:T(4,128)S(1)}, f32[4,1,20,128]{3,0,2,1:T(4,128)S(1)}, u32[]{:S(2)}, u32[]{:S(2)}) collective-permute-start(f32[4,1,20,128]{3,0,2,1:T(4,128)S(1)} %get-tuple-element.13), channel_id=1, source_target_pairs={{0,4},{4,8},{8,12},{12,16},{16,20},{20,24},{24,28},{28,0},{1,5},{5... | collective-permute-start | bytes 122888 | tf_op jit(solution)/shard_map/ppermute | solution.py:15
  16.0 10.3 %collective-permute-start.1 = (f32[4,1,20,128]{3,0,2,1:T(4,128)S(1)}, f32[4,1,20,128]{3,0,2,1:T(4,128)S(1)}, u32[]{:S(2)}, u32[]{:S(2)}) collective-permute-start(f32[4,1,20,128]{3,0,2,1:T(4,128)S(1)} %get-tuple-element.14), channel_id=1, source_target_pairs={{4,0},{8,4},{12,8},{16,12},{20,16},{24,20},{28,24},{0,28},{5,1},{9... | collective-permute-start | bytes 122888 | tf_op jit(solution)/shard_map/ppermute | solution.py:16
  20.3 3.6 %collective-permute-start.6 = (f32[1,22,1,1]{2,1,3,0:T(8,128)S(1)}, f32[1,22,1,1]{2,1,3,0:T(8,128)S(1)}, u32[]{:S(2)}, u32[]{:S(2)}) collective-permute-start(f32[1,22,1,1]{2,1,3,0:T(8,128)S(1)} %get-tuple-element.15), channel_id=1, source_target_pairs={{0,1},{1,2},{2,3},{3,0},{4,5},{5,6},{6,7},{7,4},{8,9},{9,10},{10,1... | collective-permute-start | bytes 272 | tf_op jit(solution)/shard_map/ppermute | solution.py:15
  23.1 3.1 %collective-permute-start.7 = (f32[1,22,1,1]{2,1,3,0:T(8,128)S(1)}, f32[1,22,1,1]{2,1,3,0:T(8,128)S(1)}, u32[]{:S(2)}, u32[]{:S(2)}) collective-permute-start(f32[1,22,1,1]{2,1,3,0:T(8,128)S(1)} %get-tuple-element.16), channel_id=1, source_target_pairs={{1,0},{2,1},{3,2},{0,3},{5,4},{6,5},{7,6},{4,7},{9,8},{10,9},{11,1... | collective-permute-start | bytes 272 | tf_op jit(solution)/shard_map/ppermute | solution.py:16
  26.4 1.3 %collective-permute-start.2 = (f32[4,22,1,128]{3,0,2,1:T(4,128)S(1)}, f32[4,22,1,128]{3,0,2,1:T(4,128)S(1)}, u32[]{:S(2)}, u32[]{:S(2)}) collective-permute-start(f32[4,22,1,128]{3,0,2,1:T(4,128)S(1)} %get-tuple-element.9), channel_id=1, source_target_pairs={{0,1},{1,2},{2,3},{3,0},{4,5},{5,6},{6,7},{7,4},{8,9},{9,10},{10,1... | collective-permute-start | bytes 135176 | tf_op jit(solution)/shard_map/ppermute | solution.py:15
  26.5 3.7 %collective-permute-start.3 = (f32[4,22,1,128]{3,0,2,1:T(4,128)S(1)}, f32[4,22,1,128]{3,0,2,1:T(4,128)S(1)}, u32[]{:S(2)}, u32[]{:S(2)}) collective-permute-start(f32[4,22,1,128]{3,0,2,1:T(4,128)S(1)} %get-tuple-element.10), channel_id=1, source_target_pairs={{1,0},{2,1},{3,2},{0,3},{5,4},{6,5},{7,6},{4,7},{9,8},{10,9},{11,1... | collective-permute-start | bytes 135176 | tf_op jit(solution)/shard_map/ppermute | solution.py:16
  38.9 5.6 %collective-permute-start.8 = (f32[4,1,20,128]{3,0,2,1:T(4,128)S(1)}, f32[4,1,20,128]{3,0,2,1:T(4,128)S(1)}, u32[]{:S(2)}, u32[]{:S(2)}) collective-permute-start(f32[4,1,20,128]{3,0,2,1:T(4,128)S(1)} %get-tuple-element.11), channel_id=1, source_target_pairs={{0,4},{4,8},{8,12},{12,16},{16,20},{20,24},{24,28},{28,0},{1,5},{5... | collective-permute-start | bytes 122888 | tf_op jit(solution)/shard_map/ppermute | solution.py:15
  38.9 5.5 %collective-permute-start.9 = (f32[4,1,20,128]{3,0,2,1:T(4,128)S(1)}, f32[4,1,20,128]{3,0,2,1:T(4,128)S(1)}, u32[]{:S(2)}, u32[]{:S(2)}) collective-permute-start(f32[4,1,20,128]{3,0,2,1:T(4,128)S(1)} %get-tuple-element.12), channel_id=1, source_target_pairs={{4,0},{8,4},{12,8},{16,12},{20,16},{24,20},{28,24},{0,28},{5,1},{9... | collective-permute-start | bytes 122888 | tf_op jit(solution)/shard_map/ppermute | solution.py:16
  44.5 2.3 %collective-permute-start.10 = (f32[4,22,1,128]{3,0,2,1:T(4,128)S(1)}, f32[4,22,1,128]{3,0,2,1:T(4,128)S(1)}, u32[]{:S(2)}, u32[]{:S(2)}) collective-permute-start(f32[4,22,1,128]{3,0,2,1:T(4,128)S(1)} %get-tuple-element.7), channel_id=1, source_target_pairs={{0,1},{1,2},{2,3},{3,0},{4,5},{5,6},{6,7},{7,4},{8,9},{9,10},{10,1... | collective-permute-start | bytes 135176 | tf_op jit(solution)/shard_map/ppermute | solution.py:15
  45.7 3.5 %collective-permute-start.11 = (f32[4,22,1,128]{3,0,2,1:T(4,128)S(1)}, f32[4,22,1,128]{3,0,2,1:T(4,128)S(1)}, u32[]{:S(2)}, u32[]{:S(2)}) collective-permute-start(f32[4,22,1,128]{3,0,2,1:T(4,128)S(1)} %get-tuple-element.8), channel_id=1, source_target_pairs={{1,0},{2,1},{3,2},{0,3},{5,4},{6,5},{7,6},{4,7},{9,8},{10,9},{11,1... | collective-permute-start | bytes 135176 | tf_op jit(solution)/shard_map/ppermute | solution.py:16
where the time goes:
time: 51.5 us; the launch traced here: 51.2 us
  starting transfers between devices  18 us (35%)
  matrix products  14 us (27%)
  waiting for transfers between devices  11.1 us (22%)
  local copies, waits for them, and re-layouts  4.25 us (8%)
  other arithmetic  3.59 us (7%)
    ppermute x6, starting transfers between devices, with_halo(): after = lax.ppermute(first, axis, down)  11.8 us
    ppermute x6, waiting for transfers between devices, with_halo(): after = lax.ppermute(first, axis, down)  7.12 us
    ppermute x6, starting transfers between devices, with_halo(): before = lax.ppermute(last, axis, up)  6.22 us
    ppermute x6, waiting for transfers between devices, with_halo(): before = lax.ppermute(last, axis, up)  3.99 us
    dot_general x2, matrix products, laplace(): grad_x = jnp.einsum('ab,febgcl->feagcl', table, shaped, precision=high)  3.99 us
    dot_general x2, matrix products, laplace(): weak = jnp.einsum('ba,febgcl->feagcl', table, flux_x, precision=high)  3.87 us
    dot_general x2, matrix products, laplace(): weak = weak + jnp.einsum('dc,febgdl->febgcl', table, flux_y, precision=high)  3.1 us
    dot_general x2, matrix products, laplace(): grad_y = jnp.einsum('cd,febgdl->febgcl', table, shaped, precision=high)  2.99 us
  transfers between devices with their start and end apart: 12, of which 7 were waited for; matrix products, arithmetic and copies ran while one was open for 18% of the time, Pallas kernels for 0%

commit v1 on v0

v1 whole, which is shorter than its diff:
```python
import functools

import jax
import jax.numpy as jnp
import numpy as np
from jax import lax
from jax.experimental import pallas as pl
from jax.experimental.pallas import tpu as pltpu
from jax.sharding import PartitionSpec as P

F32 = jnp.float32
VMEM = pltpu.VMEM


def derivative_table():
    small = 1.0 / np.sqrt(5.0)
    nodes = np.array([-1.0, -small, small, 1.0])
    count = nodes.shape[0]
    weights = np.array(
        [np.prod([nodes[a] - nodes[k] for k in range(count) if k != a]) for a in range(count)]
    )
    table = np.zeros((count, count))
    for a in range(count):
        for b in range(count):
            if a == b:
                table[a, b] = np.sum([1.0 / (nodes[a] - nodes[k]) for k in range(count) if k != a])
            else:
                table[a, b] = weights[a] / weights[b] / (nodes[a] - nodes[b])
    return table.astype(np.float32)


D = derivative_table()


def upper_half():
    return lax.broadcasted_iota(jnp.int32, (8, 128), 0) >= 4


def swap(v):
    return pltpu.roll(v, 4, 0)


def col_coefs(table, upper):
    def vec(low, high):
        return jnp.where(upper, float(high), float(low)).astype(F32)

    return [
        [
            (vec(table[2 * h, 2 * k], table[2 * h + 1, 2 * k + 1]),
             vec(table[2 * h, 2 * k + 1], table[2 * h + 1, 2 * k]))
            for k in range(2)
        ]
        for h in range(2)
    ]


def col_apply(coefs, pair):
    swapped = [swap(v) for v in pair]
    out = []
    for h in range(2):
        (s0, x0), (s1, x1) = coefs[h]
        out.append((s0 * pair[0] + x0 * swapped[0]) + (s1 * pair[1] + x1 * swapped[1]))
    return out


def row_apply(table, vs):
    out = []
    for a in range(4):
        terms = [float(table[a, b]) * vs[b] for b in range(4)]
        out.append((terms[0] + terms[1]) + (terms[2] + terms[3]))
    return out


def spread(ref, row, pair, upper):
    line = jnp.broadcast_to(ref[pl.ds(row, 1), :], (8, 128))
    index = jnp.where(upper, 2 * pair + 1, 2 * pair).astype(jnp.int32)
    return jnp.take_along_axis(line, index, axis=1, mode="promise_in_bounds")


def laplace_band(load, e, pairs, mets, out_ref, colf_ref, coll_ref):
    d0, d1, dx = mets
    upper = upper_half()
    lower = jnp.logical_not(upper)
    fwd = col_coefs(D, upper)
    bwd = col_coefs(-D.T, upper)
    base = 4 * e
    done = [[None] * pairs for _ in range(4)]
    for g in range(pairs // 2):
        u = [[load(base + a, a, 2 * g + h) for h in range(2)] for a in range(4)]
        gx = [row_apply(D, [u[b][h] for b in range(4)]) for h in range(2)]
        fx = [[None] * 2 for _ in range(4)]
        wy = [None] * 4
        for a in range(4):
            gy = col_apply(fwd, u[a])
            fy = [None] * 2
            for h in range(2):
                cross = spread(dx, base + a, 2 * g + h, upper)
                fx[a][h] = spread(d0, base + a, 2 * g + h, upper) * gx[h][a] + cross * gy[h]
                fy[h] = cross * gx[h][a] + spread(d1, base + a, 2 * g + h, upper) * gy[h]
            wy[a] = col_apply(bwd, fy)
        for h in range(2):
            wx = row_apply(-D.T, [fx[b][h] for b in range(4)])
            for a in range(4):
                done[a][2 * g + h] = wx[a] + wy[a][h]
        if g > 0:
            for a in range(4):
                left, right = done[a][2 * g - 1], done[a][2 * g]
                done[a][2 * g - 1] = left + jnp.where(upper, swap(right), 0.0)
                done[a][2 * g] = right + jnp.where(lower, swap(left), 0.0)
        ready = []
        if g > 0:
            ready.append(2 * g - 1)
        ready.append(2 * g)
        if g == pairs // 2 - 1:
            ready.append(2 * g + 1)
        for p in ready:
            for a in range(4):
                out_ref[base + a, p] = done[a][p]

    @pl.when(e > 0)
    def _():
        for p in range(pairs):
            total = out_ref[base - 1, p] + out_ref[base, p]
            out_ref[base - 1, p] = total
            out_ref[base, p] = total


def col_edges(out_ref, rows, pairs, colf_ref, coll_ref):
    for r in range(rows):
        colf_ref[r] = out_ref[r, 0][0:4]
        coll_ref[r] = out_ref[r, pairs - 1][4:8]


def stage_metrics(md_ref, mc_ref, s0, s1, sx):
    cols = mc_ref.shape[1]
    s0[:, 0:cols] = md_ref[:, 0, :]
    s1[:, 0:cols] = md_ref[:, 1, :]
    sx[:, 0:cols] = mc_ref[...]


def first_kernel(u_ref, md_ref, mc_ref, mass_ref, out_ref, colf_ref, coll_ref, s0, s1, sx, sm):
    rows, pairs = u_ref.shape[:2]
    cols = 2 * pairs
    stage_metrics(md_ref, mc_ref, s0, s1, sx)
    sm[...] = jnp.ones_like(sm)
    sm[:, 0:cols] = mass_ref[...]

    def band(e, carry):
        laplace_band(
            lambda row, a, p: u_ref[row, p], e, pairs, (s0, s1, sx), out_ref, colf_ref, coll_ref
        )
        return carry

    lax.fori_loop(0, rows // 4, band, 0)
    col_edges(out_ref, rows, pairs, colf_ref, coll_ref)
    for q in range(rows // 4):
        part = sm[pl.ds(4 * q, 4), :]
        colf_ref[rows + q] = part
        coll_ref[rows + q] = part


def low_only(v):
    return jnp.concatenate([v, jnp.zeros_like(v)], axis=0)


def high_only(v):
    return jnp.concatenate([jnp.zeros_like(v), v], axis=0)


def row_edges(a_first, a_last, before, after, rowf_ref, rowl_ref, rows, pairs):
    for source, dest, row in ((a_first, rowf_ref, 0), (a_last, rowl_ref, rows - 1)):
        for p in range(pairs):
            v = source[0, p]
            if p == 0:
                v = v + low_only(before[row])
            if p == pairs - 1:
                v = v + high_only(after[row])
            dest[p] = v


def edge_kernel_mass(af, al, before, after, mass_ref, rowf_ref, rowl_ref, mcol_ref, sb, sa, sm):
    rows, cols = mass_ref.shape
    pairs = cols // 2
    row_edges(af, al, before, after, rowf_ref, rowl_ref, rows, pairs)
    for q in range(rows // 4):
        sb[pl.ds(4 * q, 4), :] = before[rows + q]
        sa[pl.ds(4 * q, 4), :] = after[rows + q]
    sm[...] = jnp.ones_like(sm)
    sm[pl.ds(0, rows), 0:cols] = mass_ref[...]
    m = sm[...]
    lane = lax.broadcasted_iota(jnp.int32, m.shape, 1)
    prev = jnp.where(lane == 0, pltpu.roll(sb[...], 128 - (cols - 1), 1), pltpu.roll(m, 1, 1))
    following = jnp.where(
        lane == cols - 1, pltpu.roll(sa[...], cols - 1, 1), pltpu.roll(m, 127, 1)
    )
    m = m + jnp.where(lane % 4 == 0, prev, 0.0) + jnp.where(lane % 4 == 3, following, 0.0)
    sm[...] = m
    mcol_ref[...] = sm[pl.ds(0, rows), :]
    rowf_ref[pairs] = jnp.broadcast_to(sm[pl.ds(0, 1), :], (8, 128))
    rowl_ref[pairs] = jnp.broadcast_to(sm[pl.ds(rows - 1, 1), :], (8, 128))


def edge_kernel(af, al, before, after, rowf_ref, rowl_ref, *, rows, pairs):
    row_edges(af, al, before, after, rowf_ref, rowl_ref, rows, pairs)


def whole_point(a_ref, rb, ra, before, after, row, a, p, e, last, pairs):
    v = a_ref[row, p]
    if a == 0:
        v = v + jnp.where(e == 0, rb[p], 0.0)
    if a == 3:
        v = v + jnp.where(e == last, ra[p], 0.0)
    if p == 0:
        v = v + low_only(before[row])
    if p == pairs - 1:
        v = v + high_only(after[row])
    return v


def second_kernel(
    a_ref, before, after, rb, ra, mcol_ref, md_ref, mc_ref,
    out_ref, colf_ref, coll_ref, inv_ref, s0, s1, sx,
):
    rows, pairs = a_ref.shape[:2]
    last = rows // 4 - 1
    stage_metrics(md_ref, mc_ref, s0, s1, sx)
    upper = upper_half()
    for e in range(rows // 4 + 1):
        low = mcol_ref[pl.ds(4 * e - 1, 1), :] if e > 0 else rb[pairs, 0:1]
        high = mcol_ref[pl.ds(4 * e, 1), :] if e <= last else ra[pairs, 0:1]
        total = 1.0 / (low + high)
        if e > 0:
            inv_ref[pl.ds(4 * e - 1, 1), :] = total
        if e <= last:
            inv_ref[pl.ds(4 * e, 1), :] = total
            inv_ref[pl.ds(4 * e + 1, 2), :] = 1.0 / mcol_ref[pl.ds(4 * e + 1, 2), :]

    def band(e, carry):
        def load(row, a, p):
            v = whole_point(a_ref, rb, ra, before, after, row, a, p, e, last, pairs)
            return v * spread(inv_ref, row, p, upper)

        laplace_band(load, e, pairs, (s0, s1, sx), out_ref, colf_ref, coll_ref)
        return carry

    lax.fori_loop(0, rows // 4, band, 0)
    col_edges(out_ref, rows, pairs, colf_ref, coll_ref)


def last_kernel(a_ref, before, after, rb, ra, inv_ref, out_ref):
    rows, pairs = a_ref.shape[:2]
    last = rows // 4 - 1
    upper = upper_half()

    def band(e, carry):
        for a in range(4):
            for p in range(pairs):
                row = 4 * e + a
                v = whole_point(a_ref, rb, ra, before, after, row, a, p, e, last, pairs)
                out_ref[row, p] = v * spread(inv_ref, row, p, upper)
        return carry

    lax.fori_loop(0, rows // 4, band, 0)


def exchange(first, last, axis):
    devices = lax.axis_size(axis)
    up = [(i, (i + 1) % devices) for i in range(devices)]
    down = [(j, i) for i, j in up]
    return lax.ppermute(last, axis, up), lax.ppermute(first, axis, down)


def call(kernel, outs, scratch, cost, *args):
    return pl.pallas_call(
        kernel,
        out_shape=[jax.ShapeDtypeStruct(s, F32) for s in outs],
        in_specs=[pl.BlockSpec(memory_space=VMEM)] * len(args),
        out_specs=[pl.BlockSpec(memory_space=VMEM)] * len(outs),
        scratch_shapes=[VMEM(s, F32) for s in scratch],
        cost_estimate=pl.CostEstimate(flops=cost, bytes_accessed=cost // 4, transcendentals=0),
    )(*args)


def edge_call(kernel, outs, scratch, array, *args):
    rows, pairs = array.shape[:2]

    def whole(x):
        return pl.BlockSpec(x.shape, lambda i, n=len(x.shape): (0,) * n)

    return pl.pallas_call(
        kernel,
        grid=(1,),
        out_shape=[jax.ShapeDtypeStruct(s, F32) for s in outs],
        in_specs=[
            pl.BlockSpec((1, pairs, 8, 128), lambda i: (0, 0, 0, 0)),
            pl.BlockSpec((1, pairs, 8, 128), lambda i: (rows - 1, 0, 0, 0)),
        ] + [whole(x) for x in args],
        out_specs=[whole(jax.ShapeDtypeStruct(s, F32)) for s in outs],
        scratch_shapes=[VMEM(s, F32) for s in scratch],
    )(array, array, *args)


def shards(fields, metric_diag, metric_cross, point_mass):
    nfield, rows, cols, nlev = fields.shape
    pairs = cols // 2
    u = fields.transpose(1, 2, 0, 3).reshape(rows, pairs, 2 * nfield, nlev)
    md = metric_diag.transpose(1, 0, 2)
    full = (rows, pairs, 8, 128)
    line = (rows, 128)
    tall = ((rows + 7) // 8 * 8, 128)
    flops = 60 * rows * pairs * 8 * 128

    a1, cf, cl = call(
        first_kernel, [full] + [(rows + rows // 4, 4, 128)] * 2, [line] * 4, flops,
        u, md, metric_cross, point_mass,
    )
    cb, ca = exchange(cf, cl, "col")
    rf, rl, mcol = edge_call(
        edge_kernel_mass, [(pairs + 1, 8, 128)] * 2 + [line], [tall] * 3, a1, cb, ca, point_mass
    )
    rb, ra = exchange(rf, rl, "face")
    a2, cf, cl, inv = call(
        second_kernel, [full] + [(rows, 4, 128)] * 2 + [line], [line] * 3, flops,
        a1, cb, ca, rb, ra, mcol, md, metric_cross,
    )
    cb, ca = exchange(cf, cl, "col")
    rf, rl = edge_call(
        functools.partial(edge_kernel, rows=rows, pairs=pairs),
        [(pairs, 8, 128)] * 2, [], a2, cb, ca,
    )
    rb, ra = exchange(rf, rl, "face")
    (out,) = call(last_kernel, [full], [], flops // 10, a2, cb, ca, rb, ra, inv)
    return out.reshape(rows, cols, nfield, nlev).transpose(2, 0, 1, 3)


def solution(mesh):
    return jax.shard_map(
        shards,
        mesh=mesh,
        in_specs=(
            P(None, "face", "col", None),
            P(None, "face", "col"),
            P("face", "col"),
            P("face", "col"),
        ),
        out_specs=P(None, "face", "col", None),
        check_vma=False,
    )
```

time: 51.5 us -> 40.7 us (0.79)
  Pallas kernels: 0 us -> 14.4 us
  matrix products: 14 us -> 0 us
  starting transfers between devices: 18 us -> 12.9 us
  other arithmetic: 3.59 us -> 0 us
  local copies, waits for them, and re-layouts: 4.25 us -> 2.5 us
    pallas_call x0 -> x5, Pallas kernels: none -> 14.4 us  [the longest x3 11.3 us: call(): pl.pallas_call(kernel, out_shape=[jax.ShapeDtypeStruct(s, F32) for s in o...]
    dot_general x8 -> x0, matrix products: 14 us -> none  [the longest x2 3.99 us: laplace(): grad_x = jnp.einsum('ab,febgcl->feagcl', table, shaped, precision=high)]
    ppermute x12 -> x8, starting transfers between devices: 18 us -> 12.9 us  [exchange(): return (lax.ppermute(last, axis, up), lax.ppermute(first, axis, down))]
    div x3 -> x0, other arithmetic: 2.28 us -> none  [the longest x1 1.47 us: shards(): return assemble(padded_second) / mass_sum]
    slice x5 -> x0, local copies, waits for them, and re-layouts: 1.73 us -> none  [the longest x4 0.87 us: with_halo(): last = lax.slice_in_dim(array, length - width, length, axis=dim)]
    unnamed x8 -> x16, local copies, waits for them, and re-layouts: 0.86 us -> 2.5 us
    mul x6 -> x0, local copies, waits for them, and re-layouts: 1.02 us -> none  [the longest x4 0.68 us: laplace(): flux_x = first_diag * grad_x + cross_term * grad_y]
    add x3 -> x0, other arithmetic: 0.75 us -> none  [assemble(): padded[:, 1:-1] + row_low * padded[:, :-2] + row_high * padded[:, 2:]]
  transfers between devices with their start and end apart: 12 -> 8, of which waited for: 7 -> 6; matrix products, arithmetic and copies ran while one was open for 18% -> 0% of each run, Pallas kernels for 0% -> 0%
where the time goes in v1:
time: 40.7 us; the launch traced here: 40.4 us
  Pallas kernels  14.4 us (35%)
  starting transfers between devices  12.9 us (32%)
  waiting for transfers between devices  10.6 us (26%)
  local copies, waits for them, and re-layouts  2.5 us (6%)
    ppermute x8, starting transfers between devices, exchange(): return (lax.ppermute(last, axis, up), lax.ppermute(first, axis, down))  12.9 us
    pallas_call x3, Pallas kernels, call(): pl.pallas_call(kernel, out_shape=[jax.ShapeDtypeStruct(s, F32) for s in o...  11.3 us
    ppermute x8, waiting for transfers between devices, exchange(): return (lax.ppermute(last, axis, up), lax.ppermute(first, axis, down))  10.6 us
    pallas_call x2, Pallas kernels, edge_call(): pl.pallas_call(kernel, grid=(1,), out_shape=[jax.ShapeDtypeStruct(s, F32)...  3.07 us
    unnamed x16, local copies, waits for them, and re-layouts  2.5 us
  transfers between devices with their start and end apart: 8, of which 6 were waited for; matrix products, arithmetic and copies ran while one was open for 0% of the time, Pallas kernels for 0%

profile of v1, /device:TPU:1, one launch (start us, length us, event | category | flops | bytes accessed | tf_op | source)
XLA Modules:
  0.0 40.4 jit_solution(4369855667792050296)
XLA Ops:
  0.0 3.9 %shard_map.46 = (f32[20,10,8,128]{3,2,1,0:T(8,128)}, f32[25,4,128]{2,1,0:T(4,128)}, f32[25,4,128]{2,1,0:T(4,128)}) custom-call(f32[20,10,8,128]{3,2,1,0:T(8,128)} %bitcast.7, f32[20,2,20]{2,1,0:T(2,128)} %bitcast.8, f32[20,20]{1,0:T(8,128)} %mc_ref.3, f32[20,20]{1,0:T(8,128)} %mass_ref.3), custom_call_target="tpu_custom_call" | custom-call | flops 12288000 | bytes 3072000 | tf_op jit(solution)/shard_map/pallas_call | solution.py:274
  3.9 2.6 %collective-permute-start = (f32[25,4,128]{2,1,0:T(4,128)}, f32[25,4,128]{2,1,0:T(4,128)S(1)}, u32[]{:S(2)}, u32[]{:S(2)}) collective-permute-start(f32[25,4,128]{2,1,0:T(4,128)} %get-tuple-element.18), channel_id=1, source_target_pairs={{0,1},{1,2},{2,3},{3,0},{4,5},{5,6},{6,7},{7,4},{8,9},{9,10},{10,1... | collective-permute-start | bytes 153608 | tf_op jit(solution)/shard_map/ppermute | solution.py:270
  6.5 0.0 collective-permute-start.1
  6.5 1.9 %collective-permute-done.before = f32[25,4,128]{2,1,0:T(4,128)S(1)} collective-permute-done((f32[25,4,128]{2,1,0:T(4,128)}, f32[25,4,128]{2,1,0:T(4,128)S(1)}, u32[]{:S(2)}, u32[]{:S(2)}) %collective-permute-start) | collective-permute-done | bytes 51232 | tf_op jit(solution)/shard_map/ppermute | solution.py:270
  8.4 0.0 copy-start
  8.4 1.8 %collective-permute-done.1.after = f32[25,4,128]{2,1,0:T(4,128)S(1)} collective-permute-done((f32[25,4,128]{2,1,0:T(4,128)}, f32[25,4,128]{2,1,0:T(4,128)S(1)}, u32[]{:S(2)}, u32[]{:S(2)}) %collective-permute-start.1) | collective-permute-done | bytes 51232 | tf_op jit(solution)/shard_map/ppermute | solution.py:270
  10.2 0.0 copy-start.1
  10.2 0.0 copy-done
  10.2 0.6 %copy-done.1 = f32[25,4,128]{2,1,0:T(4,128)} copy-done((f32[25,4,128]{2,1,0:T(4,128)}, f32[25,4,128]{2,1,0:T(4,128)S(1)}, u32[]{:S(2)}) %copy-start.1) | copy-done | bytes 51224
  10.9 1.6 %shard_map.47 = (f32[11,8,128]{2,1,0:T(8,128)}, f32[11,8,128]{2,1,0:T(8,128)}, f32[20,128]{1,0:T(8,128)}) custom-call(f32[20,10,8,128]{3,2,1,0:T(8,128)} %get-tuple-element.17.af.al.a_ref, f32[20,10,8,128]{3,2,1,0:T(8,128)} %get-tuple-element.17.af.al.a_ref, f32[25,4,128]{2,1,0:T(4,128)} %copy-done, f32[25,4,128]{2,1,0:T(4,128)} %copy-done.1, f32[20,20]{1,0:T(8,128)} %mass_ref.3), custom_call_target="tpu_custom_call" | custom-call | tf_op jit(solution)/shard_map/pallas_call | solution.py:290
  12.4 1.2 %collective-permute-start.2 = (f32[11,8,128]{2,1,0:T(8,128)}, f32[11,8,128]{2,1,0:T(8,128)S(1)}, u32[]{:S(2)}, u32[]{:S(2)}) collective-permute-start(f32[11,8,128]{2,1,0:T(8,128)} %get-tuple-element.20), channel_id=1, source_target_pairs={{0,4},{4,8},{8,12},{12,16},{16,20},{20,24},{24,28},{28,0},{1,5},{5... | collective-permute-start | bytes 135176 | tf_op jit(solution)/shard_map/ppermute | solution.py:270
  13.7 3.0 %collective-permute-start.3 = (f32[11,8,128]{2,1,0:T(8,128)}, f32[11,8,128]{2,1,0:T(8,128)S(1)}, u32[]{:S(2)}, u32[]{:S(2)}) collective-permute-start(f32[11,8,128]{2,1,0:T(8,128)} %get-tuple-element.21), channel_id=1, source_target_pairs={{4,0},{8,4},{12,8},{16,12},{20,16},{24,20},{28,24},{0,28},{5,1},{9... | collective-permute-start | bytes 135176 | tf_op jit(solution)/shard_map/ppermute | solution.py:270
  16.7 1.6 %collective-permute-done.2.rb = f32[11,8,128]{2,1,0:T(8,128)S(1)} collective-permute-done((f32[11,8,128]{2,1,0:T(8,128)}, f32[11,8,128]{2,1,0:T(8,128)S(1)}, u32[]{:S(2)}, u32[]{:S(2)}) %collective-permute-start.2) | collective-permute-done | bytes 45088 | tf_op jit(solution)/shard_map/ppermute | solution.py:270
  18.4 0.0 copy-start.4
  18.4 0.0 collective-permute-done.3.ra
  18.4 0.6 %copy-done.4 = f32[11,8,128]{2,1,0:T(8,128)} copy-done((f32[11,8,128]{2,1,0:T(8,128)}, f32[11,8,128]{2,1,0:T(8,128)S(1)}, u32[]{:S(2)}) %copy-start.4) | copy-done | bytes 45080
  19.0 0.0 copy-done.5
  19.0 4.4 %shard_map.48 = (f32[20,10,8,128]{3,2,1,0:T(8,128)}, f32[20,4,128]{2,1,0:T(4,128)}, f32[20,4,128]{2,1,0:T(4,128)}, f32[20,128]{1,0:T(8,128)}) custom-call(f32[20,10,8,128]{3,2,1,0:T(8,128)} %get-tuple-element.17.af.al.a_ref, f32[25,4,128]{2,1,0:T(4,128)} %copy-done, f32[25,4,128]{2,1,0:T(4,128)} %copy-done.1, f32[11,8,128]{2,1,0:T(8,128)} %copy-done.4, ...), custom_call_target="tpu_custom_call" | custom-call | flops 12288000 | bytes 3072000 | tf_op jit(solution)/shard_map/pallas_call | solution.py:274
  23.4 1.6 %collective-permute-start.4 = (f32[20,4,128]{2,1,0:T(4,128)}, f32[20,4,128]{2,1,0:T(4,128)S(1)}, u32[]{:S(2)}, u32[]{:S(2)}) collective-permute-start(f32[20,4,128]{2,1,0:T(4,128)} %get-tuple-element.24), channel_id=1, source_target_pairs={{0,1},{1,2},{2,3},{3,0},{4,5},{5,6},{6,7},{7,4},{8,9},{9,10},{10,1... | collective-permute-start | bytes 122888 | tf_op jit(solution)/shard_map/ppermute | solution.py:270
  25.0 0.0 collective-permute-start.5
  25.0 1.5 %collective-permute-done.4.before = f32[20,4,128]{2,1,0:T(4,128)S(1)} collective-permute-done((f32[20,4,128]{2,1,0:T(4,128)}, f32[20,4,128]{2,1,0:T(4,128)S(1)}, u32[]{:S(2)}, u32[]{:S(2)}) %collective-permute-start.4) | collective-permute-done | bytes 40992 | tf_op jit(solution)/shard_map/ppermute | solution.py:270
  26.5 2.1 %collective-permute-done.5.after = f32[20,4,128]{2,1,0:T(4,128)S(1)} collective-permute-done((f32[20,4,128]{2,1,0:T(4,128)}, f32[20,4,128]{2,1,0:T(4,128)S(1)}, u32[]{:S(2)}, u32[]{:S(2)}) %collective-permute-start.5) | collective-permute-done | bytes 40992 | tf_op jit(solution)/shard_map/ppermute | solution.py:270
  28.7 0.0 copy-done.2
  28.7 0.6 %copy-done.3 = f32[20,4,128]{2,1,0:T(4,128)} copy-done((f32[20,4,128]{2,1,0:T(4,128)}, f32[20,4,128]{2,1,0:T(4,128)S(1)}, u32[]{:S(2)}) %copy-start.3) | copy-done | bytes 40984
  29.3 1.5 %shard_map.49 = (f32[10,8,128]{2,1,0:T(8,128)}, f32[10,8,128]{2,1,0:T(8,128)}) custom-call(f32[20,10,8,128]{3,2,1,0:T(8,128)} %get-tuple-element.23.af.al.a_ref, f32[20,10,8,128]{3,2,1,0:T(8,128)} %get-tuple-element.23.af.al.a_ref, f32[20,4,128]{2,1,0:T(4,128)} %copy-done.2, f32[20,4,128]{2,1,0:T(4,128)} %copy-done.3), custom_call_target="tpu_custom_call" | custom-call | tf_op jit(solution)/shard_map/pallas_call | solution.py:290
  30.8 0.5 %collective-permute-start.6 = (f32[10,8,128]{2,1,0:T(8,128)}, f32[10,8,128]{2,1,0:T(8,128)S(1)}, u32[]{:S(2)}, u32[]{:S(2)}) collective-permute-start(f32[10,8,128]{2,1,0:T(8,128)} %get-tuple-element.26), channel_id=1, source_target_pairs={{0,4},{4,8},{8,12},{12,16},{16,20},{20,24},{24,28},{28,0},{1,5},{5... | collective-permute-start | bytes 122888 | tf_op jit(solution)/shard_map/ppermute | solution.py:270
  31.2 3.9 %collective-permute-start.7 = (f32[10,8,128]{2,1,0:T(8,128)}, f32[10,8,128]{2,1,0:T(8,128)S(1)}, u32[]{:S(2)}, u32[]{:S(2)}) collective-permute-start(f32[10,8,128]{2,1,0:T(8,128)} %get-tuple-element.27), channel_id=1, source_target_pairs={{4,0},{8,4},{12,8},{16,12},{20,16},{24,20},{28,24},{0,28},{5,1},{9... | collective-permute-start | bytes 122888 | tf_op jit(solution)/shard_map/ppermute | solution.py:270
  35.2 1.6 %collective-permute-done.6.rb = f32[10,8,128]{2,1,0:T(8,128)S(1)} collective-permute-done((f32[10,8,128]{2,1,0:T(8,128)}, f32[10,8,128]{2,1,0:T(8,128)S(1)}, u32[]{:S(2)}, u32[]{:S(2)}) %collective-permute-start.6) | collective-permute-done | bytes 40992 | tf_op jit(solution)/shard_map/ppermute | solution.py:270
  36.8 0.0 collective-permute-done.7.ra
  36.8 0.6 %copy-done.6 = f32[10,8,128]{2,1,0:T(8,128)} copy-done((f32[10,8,128]{2,1,0:T(8,128)}, f32[10,8,128]{2,1,0:T(8,128)S(1)}, u32[]{:S(2)}) %copy-start.6) | copy-done | bytes 40984
  37.4 0.0 copy-done.7
  37.4 3.0 %shard_map.50 = f32[20,10,8,128]{3,2,1,0:T(8,128)} custom-call(f32[20,10,8,128]{3,2,1,0:T(8,128)} %get-tuple-element.23.af.al.a_ref, f32[20,4,128]{2,1,0:T(4,128)} %copy-done.2, f32[20,4,128]{2,1,0:T(4,128)} %copy-done.3, f32[10,8,128]{2,1,0:T(8,128)} %copy-done.6, f32[10,8,128]{2,1,0:T(8,128)} %copy-done.7, f32[20,128]{1,0:T(8,128)} %get-tuple-element.28.inv_ref), custom_call_target="tpu_custom_call" | custom-call | flops 1228800 | bytes 307200 | tf_op jit(solution)/shard_map/pallas_call | solution.py:274
  (5 shorter events, 0.0 us)
Async XLA Ops:
  3.9 4.5 %collective-permute-start = (f32[25,4,128]{2,1,0:T(4,128)}, f32[25,4,128]{2,1,0:T(4,128)S(1)}, u32[]{:S(2)}, u32[]{:S(2)}) collective-permute-start(f32[25,4,128]{2,1,0:T(4,128)} %get-tuple-element.18), channel_id=1, source_target_pairs={{0,1},{1,2},{2,3},{3,0},{4,5},{5,6},{6,7},{7,4},{8,9},{9,10},{10,1... | collective-permute-start | bytes 153608 | tf_op jit(solution)/shard_map/ppermute | solution.py:270
  6.5 3.7 %collective-permute-start.1 = (f32[25,4,128]{2,1,0:T(4,128)}, f32[25,4,128]{2,1,0:T(4,128)S(1)}, u32[]{:S(2)}, u32[]{:S(2)}) collective-permute-start(f32[25,4,128]{2,1,0:T(4,128)} %get-tuple-element.19), channel_id=1, source_target_pairs={{1,0},{2,1},{3,2},{0,3},{5,4},{6,5},{7,6},{4,7},{9,8},{10,9},{11,1... | collective-permute-start | bytes 153608 | tf_op jit(solution)/shard_map/ppermute | solution.py:270
  8.4 1.9 %copy-start = (f32[25,4,128]{2,1,0:T(4,128)}, f32[25,4,128]{2,1,0:T(4,128)S(1)}, u32[]{:S(2)}) copy-start(f32[25,4,128]{2,1,0:T(4,128)S(1)} %collective-permute-done.before) | copy-start | bytes 153604
  10.2 0.6 %copy-start.1 = (f32[25,4,128]{2,1,0:T(4,128)}, f32[25,4,128]{2,1,0:T(4,128)S(1)}, u32[]{:S(2)}) copy-start(f32[25,4,128]{2,1,0:T(4,128)S(1)} %collective-permute-done.1.after) | copy-start | bytes 153604
  12.4 5.9 %collective-permute-start.2 = (f32[11,8,128]{2,1,0:T(8,128)}, f32[11,8,128]{2,1,0:T(8,128)S(1)}, u32[]{:S(2)}, u32[]{:S(2)}) collective-permute-start(f32[11,8,128]{2,1,0:T(8,128)} %get-tuple-element.20), channel_id=1, source_target_pairs={{0,4},{4,8},{8,12},{12,16},{16,20},{20,24},{24,28},{28,0},{1,5},{5... | collective-permute-start | bytes 135176 | tf_op jit(solution)/shard_map/ppermute | solution.py:270
  13.7 4.7 %collective-permute-start.3 = (f32[11,8,128]{2,1,0:T(8,128)}, f32[11,8,128]{2,1,0:T(8,128)S(1)}, u32[]{:S(2)}, u32[]{:S(2)}) collective-permute-start(f32[11,8,128]{2,1,0:T(8,128)} %get-tuple-element.21), channel_id=1, source_target_pairs={{4,0},{8,4},{12,8},{16,12},{20,16},{24,20},{28,24},{0,28},{5,1},{9... | collective-permute-start | bytes 135176 | tf_op jit(solution)/shard_map/ppermute | solution.py:270
  18.4 0.6 %copy-start.4 = (f32[11,8,128]{2,1,0:T(8,128)}, f32[11,8,128]{2,1,0:T(8,128)S(1)}, u32[]{:S(2)}) copy-start(f32[11,8,128]{2,1,0:T(8,128)S(1)} %collective-permute-done.2.rb) | copy-start | bytes 135172
  18.4 0.6 %copy-start.5 = (f32[11,8,128]{2,1,0:T(8,128)}, f32[11,8,128]{2,1,0:T(8,128)S(1)}, u32[]{:S(2)}) copy-start(f32[11,8,128]{2,1,0:T(8,128)S(1)} %collective-permute-done.3.ra) | copy-start | bytes 135172
  23.4 3.1 %collective-permute-start.4 = (f32[20,4,128]{2,1,0:T(4,128)}, f32[20,4,128]{2,1,0:T(4,128)S(1)}, u32[]{:S(2)}, u32[]{:S(2)}) collective-permute-start(f32[20,4,128]{2,1,0:T(4,128)} %get-tuple-element.24), channel_id=1, source_target_pairs={{0,1},{1,2},{2,3},{3,0},{4,5},{5,6},{6,7},{7,4},{8,9},{9,10},{10,1... | collective-permute-start | bytes 122888 | tf_op jit(solution)/shard_map/ppermute | solution.py:270
  25.0 3.6 %collective-permute-start.5 = (f32[20,4,128]{2,1,0:T(4,128)}, f32[20,4,128]{2,1,0:T(4,128)S(1)}, u32[]{:S(2)}, u32[]{:S(2)}) collective-permute-start(f32[20,4,128]{2,1,0:T(4,128)} %get-tuple-element.25), channel_id=1, source_target_pairs={{1,0},{2,1},{3,2},{0,3},{5,4},{6,5},{7,6},{4,7},{9,8},{10,9},{11,1... | collective-permute-start | bytes 122888 | tf_op jit(solution)/shard_map/ppermute | solution.py:270
  26.5 2.1 %copy-start.2 = (f32[20,4,128]{2,1,0:T(4,128)}, f32[20,4,128]{2,1,0:T(4,128)S(1)}, u32[]{:S(2)}) copy-start(f32[20,4,128]{2,1,0:T(4,128)S(1)} %collective-permute-done.4.before) | copy-start | bytes 122884
  28.7 0.6 %copy-start.3 = (f32[20,4,128]{2,1,0:T(4,128)}, f32[20,4,128]{2,1,0:T(4,128)S(1)}, u32[]{:S(2)}) copy-start(f32[20,4,128]{2,1,0:T(4,128)S(1)} %collective-permute-done.5.after) | copy-start | bytes 122884
  30.8 6.0 %collective-permute-start.6 = (f32[10,8,128]{2,1,0:T(8,128)}, f32[10,8,128]{2,1,0:T(8,128)S(1)}, u32[]{:S(2)}, u32[]{:S(2)}) collective-permute-start(f32[10,8,128]{2,1,0:T(8,128)} %get-tuple-element.26), channel_id=1, source_target_pairs={{0,4},{4,8},{8,12},{12,16},{16,20},{20,24},{24,28},{28,0},{1,5},{5... | collective-permute-start | bytes 122888 | tf_op jit(solution)/shard_map/ppermute | solution.py:270
  31.2 5.5 %collective-permute-start.7 = (f32[10,8,128]{2,1,0:T(8,128)}, f32[10,8,128]{2,1,0:T(8,128)S(1)}, u32[]{:S(2)}, u32[]{:S(2)}) collective-permute-start(f32[10,8,128]{2,1,0:T(8,128)} %get-tuple-element.27), channel_id=1, source_target_pairs={{4,0},{8,4},{12,8},{16,12},{20,16},{24,20},{28,24},{0,28},{5,1},{9... | collective-permute-start | bytes 122888 | tf_op jit(solution)/shard_map/ppermute | solution.py:270
  36.8 0.6 %copy-start.6 = (f32[10,8,128]{2,1,0:T(8,128)}, f32[10,8,128]{2,1,0:T(8,128)S(1)}, u32[]{:S(2)}) copy-start(f32[10,8,128]{2,1,0:T(8,128)S(1)} %collective-permute-done.6.rb) | copy-start | bytes 122884
  36.8 0.6 %copy-start.7 = (f32[10,8,128]{2,1,0:T(8,128)}, f32[10,8,128]{2,1,0:T(8,128)S(1)}, u32[]{:S(2)}) copy-start(f32[10,8,128]{2,1,0:T(8,128)S(1)} %collective-permute-done.7.ra) | copy-start | bytes 122884

commit v2 on v0

v2 whole, which is shorter than its diff:
```python
import jax
import jax.numpy as jnp
import numpy as np
from jax import lax
from jax.experimental import pallas as pl
from jax.experimental.pallas import tpu as pltpu
from jax.sharding import PartitionSpec as P

F32 = jnp.float32
VMEM = pltpu.VMEM
VMEM_LIMIT = 6 * 2**20


def derivative_table():
    small = 1.0 / np.sqrt(5.0)
    nodes = np.array([-1.0, -small, small, 1.0])
    count = nodes.shape[0]
    weights = np.array(
        [np.prod([nodes[a] - nodes[k] for k in range(count) if k != a]) for a in range(count)]
    )
    table = np.zeros((count, count))
    for a in range(count):
        for b in range(count):
            if a == b:
                table[a, b] = np.sum([1.0 / (nodes[a] - nodes[k]) for k in range(count) if k != a])
            else:
                table[a, b] = weights[a] / weights[b] / (nodes[a] - nodes[b])
    return table.astype(np.float32)


D = derivative_table()


def upper_half():
    return lax.broadcasted_iota(jnp.int32, (8, 128), 0) >= 4


def swap(v):
    return pltpu.roll(v, 4, 0)


def col_coefs(table, upper):
    def vec(low, high):
        return jnp.where(upper, float(high), float(low)).astype(F32)

    return [
        [
            (vec(table[2 * h, 2 * k], table[2 * h + 1, 2 * k + 1]),
             vec(table[2 * h, 2 * k + 1], table[2 * h + 1, 2 * k]))
            for k in range(2)
        ]
        for h in range(2)
    ]


def col_apply(coefs, pair):
    swapped = [swap(v) for v in pair]
    out = []
    for h in range(2):
        (s0, x0), (s1, x1) = coefs[h]
        out.append((s0 * pair[0] + x0 * swapped[0]) + (s1 * pair[1] + x1 * swapped[1]))
    return out


def row_apply(table, vs):
    out = []
    for a in range(4):
        terms = [float(table[a, b]) * vs[b] for b in range(4)]
        out.append((terms[0] + terms[1]) + (terms[2] + terms[3]))
    return out


def spread(ref, row, pair, upper):
    line = jnp.broadcast_to(ref[pl.ds(row, 1), :], (8, 128))
    index = jnp.where(upper, 2 * pair + 1, 2 * pair).astype(jnp.int32)
    return jnp.take_along_axis(line, index, axis=1, mode="promise_in_bounds")


def element(load, base, g, mets, upper, fwd, bwd):
    d0, d1, dx = mets
    u = [[load(base + a, a, 2 * g + h) for h in range(2)] for a in range(4)]
    gx = [row_apply(D, [u[b][h] for b in range(4)]) for h in range(2)]
    fx = [[None] * 2 for _ in range(4)]
    wy = [None] * 4
    for a in range(4):
        gy = col_apply(fwd, u[a])
        fy = [None] * 2
        for h in range(2):
            p = 2 * g + h
            cross = spread(dx, base + a, p, upper)
            fx[a][h] = spread(d0, base + a, p, upper) * gx[h][a] + cross * gy[h]
            fy[h] = cross * gx[h][a] + spread(d1, base + a, p, upper) * gy[h]
        wy[a] = col_apply(bwd, fy)
    done = [[None] * 2 for _ in range(4)]
    for h in range(2):
        wx = row_apply(-D.T, [fx[b][h] for b in range(4)])
        for a in range(4):
            done[a][h] = wx[a] + wy[a][h]
    return done


def laplace_band(made, base, put, pairs, upper):
    lower = jnp.logical_not(upper)
    previous = None
    for g in range(pairs // 2):
        done = made(g)
        if previous is not None:
            for a in range(4):
                left, right = previous[a], done[a][0]
                put(base + a, 2 * g - 1, left + jnp.where(upper, swap(right), 0.0))
                done[a][0] = right + jnp.where(lower, swap(left), 0.0)
        for a in range(4):
            put(base + a, 2 * g, done[a][0])
        previous = [done[a][1] for a in range(4)]
    for a in range(4):
        put(base + a, pairs - 1, previous[a])


def join_rows(ref, row, pairs):
    for p in range(pairs):
        total = ref[row - 1, p] + ref[row, p]
        ref[row - 1, p] = total
        ref[row, p] = total


def constants():
    upper = upper_half()
    return upper, col_coefs(D, upper), col_coefs(-D.T, upper)


def odd(axis):
    return lax.rem(lax.axis_index(axis), 2) == 1


def put_slots(is_odd, index, first, last, slot_a, slot_b):
    slot_a[index] = jnp.where(is_odd, first, last)
    slot_b[index] = jnp.where(is_odd, last, first)


def first_edges(
    u_hbm, md_hbm, mc_hbm, mass_hbm,
    edge_ref, ca_ref, cb_ref, s0, s1, sx, sm, u_ref, md_v, mc_v, mass_v, sem,
):
    rows, pairs = u_ref.shape[:2]
    cols = 2 * pairs
    bands = rows // 4

    def chunk(e):
        part = pl.ds(4 * e, 4)
        return pltpu.make_async_copy(u_hbm.at[part], u_ref.at[part], sem.at[e])

    small = [
        pltpu.make_async_copy(source, dest, sem.at[bands + k])
        for k, (source, dest) in enumerate(
            ((md_hbm, md_v), (mc_hbm, mc_v), (mass_hbm, mass_v))
        )
    ]
    for copy in small:
        copy.start()
    for e in range(bands):
        chunk(e).start()
    for copy in small:
        copy.wait()
    s0[:, 0:cols] = md_v[:, 0, :]
    s1[:, 0:cols] = md_v[:, 1, :]
    sx[:, 0:cols] = mc_v[...]
    sm[...] = jnp.ones_like(sm)
    sm[:, 0:cols] = mass_v[...]
    upper, fwd, bwd = constants()

    def band(e, carry):
        chunk(e).wait()
        for k, g in enumerate((0, pairs // 2 - 1)):
            done = element(
                lambda row, a, p: u_ref[row, p], 4 * e, g, (s0, s1, sx), upper, fwd, bwd
            )
            for a in range(4):
                for h in range(2):
                    edge_ref[4 * e + a, 2 * k + h] = done[a][h]
        return carry

    lax.fori_loop(0, bands, band, 0)
    is_odd = odd("col")
    firsts = [edge_ref[r, 0] for r in range(rows)]
    lasts = [edge_ref[r, 3] for r in range(rows)]
    for r in range(rows):
        f, l = firsts[r], lasts[r]
        other = r - 1 if r % 4 == 0 else r + 1 if r % 4 == 3 else -1
        if 0 <= other < rows:
            f, l = f + firsts[other], l + lasts[other]
        put_slots(is_odd, r, f[0:4], l[4:8], ca_ref, cb_ref)
    for q in range(bands):
        part = sm[pl.ds(4 * q, 4), :]
        ca_ref[rows + q] = part
        cb_ref[rows + q] = part


def first_middle(u_ref, edge_ref, s0, s1, sx, out_ref, rowf_ref, rowl_ref):
    rows, pairs = u_ref.shape[:2]
    last = pairs // 2 - 1
    upper, fwd, bwd = constants()

    def band(e, carry):
        base = 4 * e

        def made(g):
            if g in (0, last):
                k = 0 if g == 0 else 2
                return [[edge_ref[base + a, k + h] for h in range(2)] for a in range(4)]
            return element(
                lambda row, a, p: u_ref[row, p], base, g, (s0, s1, sx), upper, fwd, bwd
            )

        def put(row, p, v):
            out_ref[row, p] = v

        laplace_band(made, base, put, pairs, upper)

        @pl.when(e > 0)
        def _():
            join_rows(out_ref, base, pairs)

        return carry

    lax.fori_loop(0, rows // 4, band, 0)
    for p in range(pairs):
        rowf_ref[p] = out_ref[0, p]
        rowl_ref[p] = out_ref[rows - 1, p]


def row_slots(rowf, rowl, ra, rb, fa_ref, fb_ref, low_ref, high_ref):
    pairs, rows = rowf.shape[0], low_ref.shape[0]
    col_odd, face_odd = odd("col"), odd("face")
    zero = jnp.zeros((4, 128), F32)
    for r in range(rows):
        a, b = ra[r], rb[r]
        low = jnp.concatenate([jnp.where(col_odd, a, b), zero], axis=0)
        high = jnp.concatenate([zero, jnp.where(col_odd, b, a)], axis=0)
        low_ref[r] = low
        high_ref[r] = high
    for p in range(pairs):
        f, l = rowf[p], rowl[p]
        if p == 0:
            f, l = f + low_ref[0], l + low_ref[rows - 1]
        if p == pairs - 1:
            f, l = f + high_ref[0], l + high_ref[rows - 1]
        put_slots(face_odd, p, f, l, fa_ref, fb_ref)


def row_slots_mass(
    rowf, rowl, ra, rb, mass, fa_ref, fb_ref, low_ref, high_ref, mcol_ref, sb, sa, sm,
):
    pairs, rows = rowf.shape[0], mass.shape[0]
    cols = 2 * pairs
    row_slots(rowf, rowl, ra, rb, fa_ref, fb_ref, low_ref, high_ref)
    col_odd = odd("col")
    for q in range(rows // 4):
        part = pl.ds(4 * q, 4)
        a, b = ra[rows + q], rb[rows + q]
        sb[part, :] = jnp.where(col_odd, a, b)
        sa[part, :] = jnp.where(col_odd, b, a)
    sm[...] = jnp.ones_like(sm)
    sm[pl.ds(0, rows), :] = mass[...]
    m = sm[...]
    lane = lax.broadcasted_iota(jnp.int32, m.shape, 1)
    prev = jnp.where(lane == 0, pltpu.roll(sb[...], 128 - (cols - 1), 1), pltpu.roll(m, 1, 1))
    following = jnp.where(
        lane == cols - 1, pltpu.roll(sa[...], cols - 1, 1), pltpu.roll(m, 127, 1)
    )
    m = m + jnp.where(lane % 4 == 0, prev, 0.0) + jnp.where(lane % 4 == 3, following, 0.0)
    sm[...] = m
    mcol_ref[...] = sm[pl.ds(0, rows), :]
    first = jnp.broadcast_to(sm[pl.ds(0, 1), :], (8, 128))
    final = jnp.broadcast_to(sm[pl.ds(rows - 1, 1), :], (8, 128))
    put_slots(odd("face"), pairs, first, final, fa_ref, fb_ref)


def with_sides(a_ref, low_ref, high_ref, row, p):
    v = a_ref[row, p]
    if p == 0:
        v = v + low_ref[row]
    if p == a_ref.shape[1] - 1:
        v = v + high_ref[row]
    return v


def second_middle(a_ref, low_ref, high_ref, mcol_ref, s0, s1, sx, out_ref, inv_ref):
    rows, pairs = a_ref.shape[:2]
    bands = rows // 4
    upper, fwd, bwd = constants()
    inv_ref[pl.ds(0, 1), :] = mcol_ref[pl.ds(0, 1), :]
    inv_ref[pl.ds(rows - 1, 1), :] = mcol_ref[pl.ds(rows - 1, 1), :]
    for e in range(bands):
        inv_ref[pl.ds(4 * e + 1, 2), :] = 1.0 / mcol_ref[pl.ds(4 * e + 1, 2), :]
        if e > 0:
            total = 1.0 / (mcol_ref[pl.ds(4 * e - 1, 1), :] + mcol_ref[pl.ds(4 * e, 1), :])
            inv_ref[pl.ds(4 * e - 1, 1), :] = total
            inv_ref[pl.ds(4 * e, 1), :] = total

    def band(e, carry):
        base = 4 * e

        def load(row, a, p):
            v = with_sides(a_ref, low_ref, high_ref, row, p)
            return v * spread(inv_ref, row, p, upper)

        def put(row, p, v):
            out_ref[row - 4, p] = v

        laplace_band(
            lambda g: element(load, base, g, (s0, s1, sx), upper, fwd, bwd),
            base, put, pairs, upper,
        )

        @pl.when(e > 1)
        def _():
            join_rows(out_ref, base - 4, pairs)

        return carry

    lax.fori_loop(1, bands - 1, band, 0)


def second_ends(
    a_ref, mid_ref, low_ref, high_ref, fa, fb, ra, rb, invm_ref, s0, s1, sx,
    out_ref, rowf_ref, rowl_ref, ca_ref, cb_ref, inv_ref, tf, tl,
):
    rows, pairs = a_ref.shape[:2]
    last = rows // 4 - 1
    upper, fwd, bwd = constants()
    face_odd = odd("face")
    for p in range(pairs + 1):
        total_a, total_b = fa[p] + ra[p], fb[p] + rb[p]
        tf[p] = jnp.where(face_odd, total_a, total_b)
        tl[p] = jnp.where(face_odd, total_b, total_a)
    inv_ref[...] = invm_ref[...]
    inv_ref[pl.ds(0, 1), :] = 1.0 / tf[pairs, 0:1]
    inv_ref[pl.ds(rows - 1, 1), :] = 1.0 / tl[pairs, 0:1]

    def band(k, carry):
        base = 4 * last * k

        def load(row, a, p):
            v = with_sides(a_ref, low_ref, high_ref, row, p)
            if a == 0:
                v = jnp.where(k == 0, tf[p], v)
            if a == 3:
                v = jnp.where(k == 1, tl[p], v)
            return v * spread(inv_ref, row, p, upper)

        def put(row, p, v):
            out_ref[row, p] = v

        laplace_band(
            lambda g: element(load, base, g, (s0, s1, sx), upper, fwd, bwd),
            base, put, pairs, upper,
        )
        return carry

    lax.fori_loop(0, 2, band, 0)

    def carry_over(r, carry):
        for p in range(pairs):
            out_ref[r, p] = mid_ref[r - 4, p]
        return carry

    lax.fori_loop(4, rows - 4, carry_over, 0)
    join_rows(out_ref, 4, pairs)
    join_rows(out_ref, rows - 4, pairs)
    for p in range(pairs):
        rowf_ref[p] = out_ref[0, p]
        rowl_ref[p] = out_ref[rows - 1, p]
    is_odd = odd("col")
    for r in range(rows):
        put_slots(is_odd, r, out_ref[r, 0][0:4], out_ref[r, pairs - 1][4:8], ca_ref, cb_ref)


def last_middle(a_ref, low_ref, high_ref, inv_ref, out_hbm, buf, sem):
    rows, pairs = a_ref.shape[:2]
    bands = rows // 4
    upper = upper_half()
    copies = []
    for e in range(bands):
        start = 1 if e == 0 else 4 * e
        stop = rows - 1 if e == bands - 1 else 4 * e + 4
        for row in range(start, stop):
            for p in range(pairs):
                v = with_sides(a_ref, low_ref, high_ref, row, p)
                buf[row, p] = v * spread(inv_ref, row, p, upper)
        part = pl.ds(start, stop - start)
        copies.append(pltpu.make_async_copy(buf.at[part], out_hbm.at[part], sem.at[e]))
        copies[-1].start()
    for copy in copies:
        copy.wait()


def last_ends(held, fa, fb, ra, rb, inv_ref, out_hbm, buf, sem):
    rows, pairs = out_hbm.shape[:2]
    upper = upper_half()
    face_odd = odd("face")
    for p in range(pairs):
        total_a, total_b = fa[p] + ra[p], fb[p] + rb[p]
        buf[0, p] = jnp.where(face_odd, total_a, total_b) * spread(inv_ref, 0, p, upper)
        buf[1, p] = jnp.where(face_odd, total_b, total_a) * spread(inv_ref, rows - 1, p, upper)
    copies = [
        pltpu.make_async_copy(buf.at[k], out_hbm.at[row], sem.at[k])
        for k, row in enumerate((0, rows - 1))
    ]
    for copy in copies:
        copy.start()
    for copy in copies:
        copy.wait()


def exchange(slot_a, slot_b, axis):
    n = lax.axis_size(axis)
    pairs_a = [(i, i ^ 1) for i in range(n)]
    pairs_b = [(i, (i + 1) % n if i % 2 else (i - 1) % n) for i in range(n)]
    got_b = lax.ppermute(slot_b, axis, pairs_b)
    got_a = lax.ppermute(slot_a, axis, pairs_a)
    return got_a, got_b


def call(kernel, outs, cost, args, scratch=(), far_in=0, far_out=False, alias=None):
    far = pl.BlockSpec(memory_space=pltpu.HBM)
    return pl.pallas_call(
        kernel,
        out_shape=[jax.ShapeDtypeStruct(s, F32) for s in outs],
        in_specs=[far] * far_in + [pl.BlockSpec()] * (len(args) - far_in),
        out_specs=[far if far_out else pl.BlockSpec()] * len(outs),
        scratch_shapes=scratch,
        input_output_aliases=alias or {},
        cost_estimate=pl.CostEstimate(flops=cost, bytes_accessed=cost // 4, transcendentals=0),
        compiler_params=pltpu.CompilerParams(vmem_limit_bytes=VMEM_LIMIT),
    )(*args)


def shards(fields, metric_diag, metric_cross, point_mass):
    nfield, rows, cols, nlev = fields.shape
    pairs, bands = cols // 2, rows // 4
    u = fields.transpose(1, 2, 0, 3).reshape(rows, pairs, 2 * nfield, nlev)
    md = metric_diag.transpose(1, 0, 2)
    full = (rows, pairs, 8, 128)
    edge = (pairs, 8, 128)
    heavy = (pairs + 1, 8, 128)
    side = (rows, 8, 128)
    line = (rows, 128)
    tall = ((rows + 7) // 8 * 8, 128)
    flops = 60 * rows * pairs * 8 * 128

    ends, ca, cb, s0, s1, sx, sm, uv = call(
        first_edges,
        [(rows, 4, 8, 128)] + [(rows + bands, 4, 128)] * 2 + [line] * 4 + [full],
        flops * 2 // 5,
        [u, md, metric_cross, point_mass],
        [VMEM(md.shape, F32), VMEM((rows, cols), F32), VMEM((rows, cols), F32),
         pltpu.SemaphoreType.DMA((bands + 3,))],
        far_in=4,
    )
    ga, gb = exchange(ca, cb, "col")
    a1, rf, rl = call(first_middle, [full, edge, edge], flops * 3 // 5, [uv, ends, s0, s1, sx])
    fa, fb, low, high, mcol = call(
        row_slots_mass, [heavy, heavy, side, side, line], flops // 50,
        [rf, rl, ga, gb, sm], [VMEM(tall, F32)] * 3,
    )
    ra, rb = exchange(fa, fb, "face")
    mid, invm = call(
        second_middle, [(rows - 8, pairs, 8, 128), line], flops * 3 // 5,
        [a1, low, high, mcol, s0, s1, sx],
    )
    a2, rf, rl, ca, cb, inv = call(
        second_ends, [full, edge, edge, (rows, 4, 128), (rows, 4, 128), line], flops * 2 // 5,
        [a1, mid, low, high, fa, fb, ra, rb, invm, s0, s1, sx], [VMEM(heavy, F32)] * 2,
    )
    ga, gb = exchange(ca, cb, "col")
    fa, fb, low, high = call(
        row_slots, [edge, edge, side, side], flops // 50, [rf, rl, ga, gb]
    )
    ra, rb = exchange(fa, fb, "face")
    (out,) = call(
        last_middle, [full], flops // 5, [a2, low, high, inv],
        [VMEM(full, F32), pltpu.SemaphoreType.DMA((bands,))], far_out=True,
    )
    (out,) = call(
        last_ends, [full], flops // 50, [out, fa, fb, ra, rb, inv],
        [VMEM((2,) + edge, F32), pltpu.SemaphoreType.DMA((2,))],
        far_in=1, far_out=True, alias={0: 0},
    )
    return out.reshape(rows, cols, nfield, nlev).transpose(2, 0, 1, 3)


def solution(mesh):
    return jax.shard_map(
        shards,
        mesh=mesh,
        in_specs=(
            P(None, "face", "col", None),
            P(None, "face", "col"),
            P("face", "col"),
            P("face", "col"),
        ),
        out_specs=P(None, "face", "col", None),
        check_vma=False,
    )
```

time: 51.5 us -> 31.5 us (0.61)
  the two profiles are of different devices: /device:TPU:1 before, /device:TPU:0 now
where the time goes in v2:
time: 31.5 us; the launch traced here: 31.2 us
  starting transfers between devices  13.6 us (43%)
  Pallas kernels  7.81 us (25%)
  waiting for transfers between devices  6.42 us (20%)
  local copies, waits for them, and re-layouts  3.28 us (10%)
    ppermute x4, starting transfers between devices, exchange(): got_b = lax.ppermute(slot_b, axis, pairs_b)  11.3 us
    pallas_call x8, Pallas kernels, call(): pl.pallas_call(kernel, out_shape=[jax.ShapeDtypeStruct(s, F32) for s in o...  7.81 us
    ppermute x4, waiting for transfers between devices, exchange(): got_b = lax.ppermute(slot_b, axis, pairs_b)  6.41 us
    unnamed x8, local copies, waits for them, and re-layouts  3.28 us
    ppermute x4, starting transfers between devices, exchange(): got_a = lax.ppermute(slot_a, axis, pairs_a)  2.22 us
  transfers between devices with their start and end apart: 8, of which 4 were waited for; matrix products, arithmetic and copies ran while one was open for 0% of the time, Pallas kernels for 12%

profile of v2, /device:TPU:0, one launch (start us, length us, event | category | flops | bytes accessed | tf_op | source)
XLA Modules:
  0.0 31.2 jit_solution(14387368627972516193)
XLA Ops:
  0.0 0.0 copy-start
  0.0 1.1 %copy-done = f32[4,20,20,128]{3,0,2,1:T(4,128)S(1)} copy-done((f32[4,20,20,128]{3,0,2,1:T(4,128)S(1)}, f32[4,20,20,128]{3,0,2,1:T(4,128)}, u32[]{:S(2)}) %copy-start) | copy-done | bytes 819224
  1.1 0.0 copy-start.1
  1.1 0.7 %copy-done.1 = f32[2,20,20]{2,0,1:T(2,128)S(1)} copy-done((f32[2,20,20]{2,0,1:T(2,128)S(1)}, f32[2,20,20]{2,0,1:T(2,128)}, u32[]{:S(2)}) %copy-start.1) | copy-done | bytes 3224
  1.9 0.0 copy-start.2
  1.9 0.7 %copy-done.2 = f32[20,20]{1,0:T(8,128)S(1)} copy-done((f32[20,20]{1,0:T(8,128)S(1)}, f32[20,20]{1,0:T(8,128)}, u32[]{:S(2)}) %copy-start.2) | copy-done | bytes 1624
  2.6 0.0 copy-start.3
  2.6 0.7 %copy-done.3 = f32[20,20]{1,0:T(8,128)S(1)} copy-done((f32[20,20]{1,0:T(8,128)S(1)}, f32[20,20]{1,0:T(8,128)}, u32[]{:S(2)}) %copy-start.3) | copy-done | bytes 1624
  3.3 2.1 %shard_map.46 = (f32[20,4,8,128]{3,2,1,0:T(8,128)S(1)}, f32[25,4,128]{2,1,0:T(4,128)S(1)}, f32[25,4,128]{2,1,0:T(4,128)S(1)}, f32[20,128]{1,0:T(8,128)S(1)}, f32...) custom-call(f32[20,10,8,128]{3,2,1,0:T(8,128)S(1)} %bitcast.7, ...), custom_call_target="tpu_custom_call" | custom-call | flops 4915200 | bytes 1228800 | tf_op jit(solution)/shard_map/pallas_call | solution.py:426
  5.4 0.6 %collective-permute-start = (f32[25,4,128]{2,1,0:T(4,128)S(1)}, f32[25,4,128]{2,1,0:T(4,128)S(1)}, u32[]{:S(2)}, u32[]{:S(2)}) collective-permute-start(f32[25,4,128]{2,1,0:T(4,128)S(1)} %get-tuple-element.41), channel_id=1, source_target_pairs={{0,1},{1,0},{2,3},{3,2},{4,5},{5,4},{6,7},{7,6},{8,9},{9,8},{10,11... | collective-permute-start | bytes 153608 | tf_op jit(solution)/shard_map/ppermute | solution.py:420
  5.9 2.6 %collective-permute-start.1 = (f32[25,4,128]{2,1,0:T(4,128)S(1)}, f32[25,4,128]{2,1,0:T(4,128)S(1)}, u32[]{:S(2)}, u32[]{:S(2)}) collective-permute-start(f32[25,4,128]{2,1,0:T(4,128)S(1)} %get-tuple-element.42), channel_id=1, source_target_pairs={{0,3},{1,2},{2,1},{3,0},{4,7},{5,6},{6,5},{7,4},{8,11},{9,10},{10,... | collective-permute-start | bytes 153608 | tf_op jit(solution)/shard_map/ppermute | solution.py:419
  8.5 1.3 %shard_map.47 = (f32[20,10,8,128]{3,2,1,0:T(8,128)S(1)}, f32[10,8,128]{2,1,0:T(8,128)S(1)}, f32[10,8,128]{2,1,0:T(8,128)S(1)}) custom-call(f32[20,10,8,128]{3,2,1,0:T(8,128)S(1)} %get-tuple-element.33.u_ref, f32[20,4,8,128]{3,2,1,0:T(8,128)S(1)} %get-tuple-element.34.edge_ref, f32[20,128]{1,0:T(8,128)S(1)} %get-tuple-element.35.s0, ...), custom_call_target="tpu_custom_call" | custom-call | flops 7372800 | bytes 1843200 | tf_op jit(solution)/shard_map/pallas_call | solution.py:426
  9.8 0.0 collective-permute-done.ra
  9.8 0.8 %collective-permute-done.1.rb = f32[25,4,128]{2,1,0:T(4,128)S(1)} collective-permute-done((f32[25,4,128]{2,1,0:T(4,128)S(1)}, f32[25,4,128]{2,1,0:T(4,128)S(1)}, u32[]{:S(2)}, u32[]{:S(2)}) %collective-permute-start.1) | collective-permute-done | bytes 51232 | tf_op jit(solution)/shard_map/ppermute | solution.py:419
  10.6 0.1 shard_map.48
  10.7 1.5 %collective-permute-start.2 = (f32[11,8,128]{2,1,0:T(8,128)S(1)}, f32[11,8,128]{2,1,0:T(8,128)S(1)}, u32[]{:S(2)}, u32[]{:S(2)}) collective-permute-start(f32[11,8,128]{2,1,0:T(8,128)S(1)} %get-tuple-element.48.fa), channel_id=1, source_target_pairs={{0,4},{4,0},{8,12},{12,8},{16,20},{20,16},{24,28},{28,24},{1,5},{5... | collective-permute-start | bytes 135176 | tf_op jit(solution)/shard_map/ppermute | solution.py:420
  12.2 3.5 %collective-permute-start.3 = (f32[11,8,128]{2,1,0:T(8,128)S(1)}, f32[11,8,128]{2,1,0:T(8,128)S(1)}, u32[]{:S(2)}, u32[]{:S(2)}) collective-permute-start(f32[11,8,128]{2,1,0:T(8,128)S(1)} %get-tuple-element.49.fb), channel_id=1, source_target_pairs={{0,28},{4,8},{8,4},{12,16},{16,12},{20,24},{24,20},{28,0},{1,29},{... | collective-permute-start | bytes 135176 | tf_op jit(solution)/shard_map/ppermute | solution.py:419
  15.8 1.3 %shard_map.49 = (f32[12,10,8,128]{3,2,1,0:T(8,128)S(1)}, f32[20,128]{1,0:T(8,128)S(1)}) custom-call(f32[20,10,8,128]{3,2,1,0:T(8,128)S(1)} %get-tuple-element.38.a_ref, f32[20,8,128]{2,1,0:T(8,128)S(1)} %get-tuple-element.44.low_ref, f32[20,8,128]{2,1,0:T(8,128)S(1)} %get-tuple-element.45.high_ref, f32[20,128]{1,0:T(8,128)S(1)} %get-tuple-element.46.mcol_ref, ...), custom_call_target="tpu_custom_call" | custom-call | flops 7372800 | bytes 1843200 | tf_op jit(solution)/shard_map/pallas_call | solution.py:426
  17.1 0.0 collective-permute-done.2.ra
  17.1 1.9 %collective-permute-done.3.rb = f32[11,8,128]{2,1,0:T(8,128)S(1)} collective-permute-done((f32[11,8,128]{2,1,0:T(8,128)S(1)}, f32[11,8,128]{2,1,0:T(8,128)S(1)}, u32[]{:S(2)}, u32[]{:S(2)}) %collective-permute-start.3) | collective-permute-done | bytes 45088 | tf_op jit(solution)/shard_map/ppermute | solution.py:419
  19.0 1.0 %shard_map.50 = (f32[20,10,8,128]{3,2,1,0:T(8,128)S(1)}, f32[10,8,128]{2,1,0:T(8,128)S(1)}, f32[10,8,128]{2,1,0:T(8,128)S(1)}, f32[20,4,128]{2,1,0:T(4,128)S(1)}...) custom-call(f32[20,10,8,128]{3,2,1,0:T(8,128)S(1)} %get-tuple-element.38.a_ref, ...), custom_call_target="tpu_custom_call" | custom-call | flops 4915200 | bytes 1228800 | tf_op jit(solution)/shard_map/pallas_call | solution.py:426
  20.0 0.1 collective-permute-start.4
  20.0 1.6 %collective-permute-start.5 = (f32[20,4,128]{2,1,0:T(4,128)S(1)}, f32[20,4,128]{2,1,0:T(4,128)S(1)}, u32[]{:S(2)}, u32[]{:S(2)}) collective-permute-start(f32[20,4,128]{2,1,0:T(4,128)S(1)} %get-tuple-element.55), channel_id=1, source_target_pairs={{0,3},{1,2},{2,1},{3,0},{4,7},{5,6},{6,5},{7,4},{8,11},{9,10},{10,... | collective-permute-start | bytes 122888 | tf_op jit(solution)/shard_map/ppermute | solution.py:419
  21.6 0.0 collective-permute-done.4.ra
  21.6 1.9 %collective-permute-done.5.rb = f32[20,4,128]{2,1,0:T(4,128)S(1)} collective-permute-done((f32[20,4,128]{2,1,0:T(4,128)S(1)}, f32[20,4,128]{2,1,0:T(4,128)S(1)}, u32[]{:S(2)}, u32[]{:S(2)}) %collective-permute-start.5) | collective-permute-done | bytes 40992 | tf_op jit(solution)/shard_map/ppermute | solution.py:419
  23.6 0.1 collective-permute-start.6
  23.6 3.6 %collective-permute-start.7 = (f32[10,8,128]{2,1,0:T(8,128)S(1)}, f32[10,8,128]{2,1,0:T(8,128)S(1)}, u32[]{:S(2)}, u32[]{:S(2)}) collective-permute-start(f32[10,8,128]{2,1,0:T(8,128)S(1)} %get-tuple-element.60.fb), channel_id=1, source_target_pairs={{0,28},{4,8},{8,4},{12,16},{16,12},{20,24},{24,20},{28,0},{1,29},{... | collective-permute-start | bytes 122888 | tf_op jit(solution)/shard_map/ppermute | solution.py:419
  27.2 1.3 %shard_map.52.held = f32[20,10,8,128]{3,2,1,0:T(8,128)} custom-call(f32[20,10,8,128]{3,2,1,0:T(8,128)S(1)} %get-tuple-element.51.a_ref, f32[20,8,128]{2,1,0:T(8,128)S(1)} %get-tuple-element.56.low_ref, f32[20,8,128]{2,1,0:T(8,128)S(1)} %get-tuple-element.57.high_ref, f32[20,128]{1,0:T(8,128)S(1)} %get-tuple-element.58.inv_ref), custom_call_target="tpu_custom_call" | custom-call | flops 2457600 | bytes 614400 | tf_op jit(solution)/shard_map/pallas_call | solution.py:426
  28.5 0.0 collective-permute-done.6.ra
  28.5 1.9 %collective-permute-done.7.rb = f32[10,8,128]{2,1,0:T(8,128)S(1)} collective-permute-done((f32[10,8,128]{2,1,0:T(8,128)S(1)}, f32[10,8,128]{2,1,0:T(8,128)S(1)}, u32[]{:S(2)}, u32[]{:S(2)}) %collective-permute-start.7) | collective-permute-done | bytes 40992 | tf_op jit(solution)/shard_map/ppermute | solution.py:419
  30.4 0.8 %shard_map.53 = f32[20,10,8,128]{3,2,1,0:T(8,128)} custom-call(f32[20,10,8,128]{3,2,1,0:T(8,128)} %shard_map.52.held, f32[10,8,128]{2,1,0:T(8,128)S(1)} %get-tuple-element.59.fa, f32[10,8,128]{2,1,0:T(8,128)S(1)} %get-tuple-element.60.fb, f32[10,8,128]{2,1,0:T(8,128)S(1)} %collective-permute-done.6.ra, ...), custom_call_target="tpu_custom_call", output_to_operand_aliasing={{}: (0, {})} | custom-call | flops 245760 | bytes 61440 | tf_op jit(solution)/shard_map/pallas_call | solution.py:426
  (1 shorter events, 0.0 us)
Async XLA Ops:
  0.0 1.1 %copy-start = (f32[4,20,20,128]{3,0,2,1:T(4,128)S(1)}, f32[4,20,20,128]{3,0,2,1:T(4,128)}, u32[]{:S(2)}) copy-start(f32[4,20,20,128]{3,0,2,1:T(4,128)} %param.4) | copy-start | bytes 2457604
  1.1 0.7 %copy-start.1 = (f32[2,20,20]{2,0,1:T(2,128)S(1)}, f32[2,20,20]{2,0,1:T(2,128)}, u32[]{:S(2)}) copy-start(f32[2,20,20]{2,0,1:T(2,128)} %param.5) | copy-start | bytes 9604
  1.9 0.7 %copy-start.2 = (f32[20,20]{1,0:T(8,128)S(1)}, f32[20,20]{1,0:T(8,128)}, u32[]{:S(2)}) copy-start(f32[20,20]{1,0:T(8,128)} %mc_hbm.1) | copy-start | bytes 4804
  2.6 0.7 %copy-start.3 = (f32[20,20]{1,0:T(8,128)S(1)}, f32[20,20]{1,0:T(8,128)}, u32[]{:S(2)}) copy-start(f32[20,20]{1,0:T(8,128)} %mass_hbm.1) | copy-start | bytes 4804
  5.4 4.4 %collective-permute-start = (f32[25,4,128]{2,1,0:T(4,128)S(1)}, f32[25,4,128]{2,1,0:T(4,128)S(1)}, u32[]{:S(2)}, u32[]{:S(2)}) collective-permute-start(f32[25,4,128]{2,1,0:T(4,128)S(1)} %get-tuple-element.41), channel_id=1, source_target_pairs={{0,1},{1,0},{2,3},{3,2},{4,5},{5,4},{6,7},{7,6},{8,9},{9,8},{10,11... | collective-permute-start | bytes 153608 | tf_op jit(solution)/shard_map/ppermute | solution.py:420
  5.9 4.7 %collective-permute-start.1 = (f32[25,4,128]{2,1,0:T(4,128)S(1)}, f32[25,4,128]{2,1,0:T(4,128)S(1)}, u32[]{:S(2)}, u32[]{:S(2)}) collective-permute-start(f32[25,4,128]{2,1,0:T(4,128)S(1)} %get-tuple-element.42), channel_id=1, source_target_pairs={{0,3},{1,2},{2,1},{3,0},{4,7},{5,6},{6,5},{7,4},{8,11},{9,10},{10,... | collective-permute-start | bytes 153608 | tf_op jit(solution)/shard_map/ppermute | solution.py:419
  10.7 6.4 %collective-permute-start.2 = (f32[11,8,128]{2,1,0:T(8,128)S(1)}, f32[11,8,128]{2,1,0:T(8,128)S(1)}, u32[]{:S(2)}, u32[]{:S(2)}) collective-permute-start(f32[11,8,128]{2,1,0:T(8,128)S(1)} %get-tuple-element.48.fa), channel_id=1, source_target_pairs={{0,4},{4,0},{8,12},{12,8},{16,20},{20,16},{24,28},{28,24},{1,5},{5... | collective-permute-start | bytes 135176 | tf_op jit(solution)/shard_map/ppermute | solution.py:420
  12.2 6.7 %collective-permute-start.3 = (f32[11,8,128]{2,1,0:T(8,128)S(1)}, f32[11,8,128]{2,1,0:T(8,128)S(1)}, u32[]{:S(2)}, u32[]{:S(2)}) collective-permute-start(f32[11,8,128]{2,1,0:T(8,128)S(1)} %get-tuple-element.49.fb), channel_id=1, source_target_pairs={{0,28},{4,8},{8,4},{12,16},{16,12},{20,24},{24,20},{28,0},{1,29},{... | collective-permute-start | bytes 135176 | tf_op jit(solution)/shard_map/ppermute | solution.py:419
  20.0 1.7 %collective-permute-start.4 = (f32[20,4,128]{2,1,0:T(4,128)S(1)}, f32[20,4,128]{2,1,0:T(4,128)S(1)}, u32[]{:S(2)}, u32[]{:S(2)}) collective-permute-start(f32[20,4,128]{2,1,0:T(4,128)S(1)} %get-tuple-element.54), channel_id=1, source_target_pairs={{0,1},{1,0},{2,3},{3,2},{4,5},{5,4},{6,7},{7,6},{8,9},{9,8},{10,11... | collective-permute-start | bytes 122888 | tf_op jit(solution)/shard_map/ppermute | solution.py:420
  20.0 3.5 %collective-permute-start.5 = (f32[20,4,128]{2,1,0:T(4,128)S(1)}, f32[20,4,128]{2,1,0:T(4,128)S(1)}, u32[]{:S(2)}, u32[]{:S(2)}) collective-permute-start(f32[20,4,128]{2,1,0:T(4,128)S(1)} %get-tuple-element.55), channel_id=1, source_target_pairs={{0,3},{1,2},{2,1},{3,0},{4,7},{5,6},{6,5},{7,4},{8,11},{9,10},{10,... | collective-permute-start | bytes 122888 | tf_op jit(solution)/shard_map/ppermute | solution.py:419
  23.6 5.0 %collective-permute-start.6 = (f32[10,8,128]{2,1,0:T(8,128)S(1)}, f32[10,8,128]{2,1,0:T(8,128)S(1)}, u32[]{:S(2)}, u32[]{:S(2)}) collective-permute-start(f32[10,8,128]{2,1,0:T(8,128)S(1)} %get-tuple-element.59.fa), channel_id=1, source_target_pairs={{0,4},{4,0},{8,12},{12,8},{16,20},{20,16},{24,28},{28,24},{1,5},{5... | collective-permute-start | bytes 122888 | tf_op jit(solution)/shard_map/ppermute | solution.py:420
  23.6 6.8 %collective-permute-start.7 = (f32[10,8,128]{2,1,0:T(8,128)S(1)}, f32[10,8,128]{2,1,0:T(8,128)S(1)}, u32[]{:S(2)}, u32[]{:S(2)}) collective-permute-start(f32[10,8,128]{2,1,0:T(8,128)S(1)} %get-tuple-element.60.fb), channel_id=1, source_target_pairs={{0,28},{4,8},{8,4},{12,16},{16,12},{20,24},{24,20},{28,0},{1,29},{... | collective-permute-start | bytes 122888 | tf_op jit(solution)/shard_map/ppermute | solution.py:419

commit v3 on v2

--- a/solution.py
+++ b/solution.py
@@ -228,7 +228,7 @@
         rowl_ref[p] = out_ref[rows - 1, p]
 
 
-def row_slots(rowf, rowl, ra, rb, fa_ref, fb_ref, low_ref, high_ref):
+def row_slots(rowf, rowl, rb, ra, fb_ref, fa_ref, low_ref, high_ref):
     pairs, rows = rowf.shape[0], low_ref.shape[0]
     col_odd, face_odd = odd("col"), odd("face")
     zero = jnp.zeros((4, 128), F32)
@@ -248,11 +248,11 @@
 
 
 def row_slots_mass(
-    rowf, rowl, ra, rb, mass, fa_ref, fb_ref, low_ref, high_ref, mcol_ref, sb, sa, sm,
+    rowf, rowl, rb, ra, mass, fb_ref, fa_ref, low_ref, high_ref, mcol_ref, sb, sa, sm,
 ):
     pairs, rows = rowf.shape[0], mass.shape[0]
     cols = 2 * pairs
-    row_slots(rowf, rowl, ra, rb, fa_ref, fb_ref, low_ref, high_ref)
+    row_slots(rowf, rowl, rb, ra, fb_ref, fa_ref, low_ref, high_ref)
     col_odd = odd("col")
     for q in range(rows // 4):
         part = pl.ds(4 * q, 4)
@@ -322,7 +322,7 @@
 
 
 def second_ends(
-    a_ref, mid_ref, low_ref, high_ref, fa, fb, ra, rb, invm_ref, s0, s1, sx,
+    a_ref, mid_ref, low_ref, high_ref, fb, fa, rb, ra, invm_ref, s0, s1, sx,
     out_ref, rowf_ref, rowl_ref, ca_ref, cb_ref, inv_ref, tf, tl,
 ):
     rows, pairs = a_ref.shape[:2]
@@ -394,7 +394,7 @@
         copy.wait()
 
 
-def last_ends(held, fa, fb, ra, rb, inv_ref, out_hbm, buf, sem):
+def last_ends(held, fb, fa, rb, ra, inv_ref, out_hbm, buf, sem):
     rows, pairs = out_hbm.shape[:2]
     upper = upper_half()
     face_odd = odd("face")
@@ -452,16 +452,17 @@
         first_edges,
         [(rows, 4, 8, 128)] + [(rows + bands, 4, 128)] * 2 + [line] * 4 + [full],
         flops * 2 // 5,
-        [u, md, metric_cross, point_mass],
+        [pltpu.with_memory_space_constraint(x, pltpu.HBM)
+         for x in (u, md, metric_cross, point_mass)],
         [VMEM(md.shape, F32), VMEM((rows, cols), F32), VMEM((rows, cols), F32),
          pltpu.SemaphoreType.DMA((bands + 3,))],
         far_in=4,
     )
     ga, gb = exchange(ca, cb, "col")
     a1, rf, rl = call(first_middle, [full, edge, edge], flops * 3 // 5, [uv, ends, s0, s1, sx])
-    fa, fb, low, high, mcol = call(
+    fb, fa, low, high, mcol = call(
         row_slots_mass, [heavy, heavy, side, side, line], flops // 50,
-        [rf, rl, ga, gb, sm], [VMEM(tall, F32)] * 3,
+        [rf, rl, gb, ga, sm], [VMEM(tall, F32)] * 3,
     )
     ra, rb = exchange(fa, fb, "face")
     mid, invm = call(
@@ -470,11 +471,11 @@
     )
     a2, rf, rl, ca, cb, inv = call(
         second_ends, [full, edge, edge, (rows, 4, 128), (rows, 4, 128), line], flops * 2 // 5,
-        [a1, mid, low, high, fa, fb, ra, rb, invm, s0, s1, sx], [VMEM(heavy, F32)] * 2,
+        [a1, mid, low, high, fb, fa, rb, ra, invm, s0, s1, sx], [VMEM(heavy, F32)] * 2,
     )
     ga, gb = exchange(ca, cb, "col")
-    fa, fb, low, high = call(
-        row_slots, [edge, edge, side, side], flops // 50, [rf, rl, ga, gb]
+    fb, fa, low, high = call(
+        row_slots, [edge, edge, side, side], flops // 50, [rf, rl, gb, ga]
     )
     ra, rb = exchange(fa, fb, "face")
     (out,) = call(
@@ -482,7 +483,7 @@
         [VMEM(full, F32), pltpu.SemaphoreType.DMA((bands,))], far_out=True,
     )
     (out,) = call(
-        last_ends, [full], flops // 50, [out, fa, fb, ra, rb, inv],
+        last_ends, [full], flops // 50, [out, fb, fa, rb, ra, inv],
         [VMEM((2,) + edge, F32), pltpu.SemaphoreType.DMA((2,))],
         far_in=1, far_out=True, alias={0: 0},
     )

time: 31.5 us -> 29.3 us (0.930)
  local copies, waits for them, and re-layouts: 3.28 us -> 0 us
  waiting for transfers between devices: 6.42 us -> 8.24 us
  starting transfers between devices: 13.6 us -> 13.2 us
    unnamed x8 -> x0, local copies, waits for them, and re-layouts: 3.28 us -> none
    ppermute x4, waiting for transfers between devices: 0.01 us -> 2.46 us  [exchange(): got_a = lax.ppermute(slot_a, axis, pairs_a)]
    ppermute x4, waiting for transfers between devices: 6.41 us -> 5.77 us  [exchange(): got_b = lax.ppermute(slot_b, axis, pairs_b)]
    ppermute x4, starting transfers between devices: 11.3 us -> 10.9 us  [exchange(): got_b = lax.ppermute(slot_b, axis, pairs_b)]
  transfers between devices with their start and end apart: 8 -> 8, of which waited for: 4 -> 6; matrix products, arithmetic and copies ran while one was open for 0% -> 0% of each run, Pallas kernels for 12% -> 13%
where the time goes in v3:
time: 29.3 us; the launch traced here: 29.2 us
  starting transfers between devices  13.2 us (45%)
  waiting for transfers between devices  8.24 us (28%)
  Pallas kernels  7.68 us (26%)
    ppermute x4, starting transfers between devices, exchange(): got_b = lax.ppermute(slot_b, axis, pairs_b)  10.9 us
    pallas_call x8, Pallas kernels, call(): pl.pallas_call(kernel, out_shape=[jax.ShapeDtypeStruct(s, F32) for s in o...  7.68 us
    ppermute x4, waiting for transfers between devices, exchange(): got_b = lax.ppermute(slot_b, axis, pairs_b)  5.77 us
    ppermute x4, waiting for transfers between devices, exchange(): got_a = lax.ppermute(slot_a, axis, pairs_a)  2.46 us
    ppermute x4, starting transfers between devices, exchange(): got_a = lax.ppermute(slot_a, axis, pairs_a)  2.31 us
  transfers between devices with their start and end apart: 8, of which 6 were waited for; matrix products, arithmetic and copies ran while one was open for 0% of the time, Pallas kernels for 13%

profile of v3, /device:TPU:0, one launch (start us, length us, event | category | flops | bytes accessed | tf_op | source)
XLA Modules:
  0.0 29.2 jit_solution(11525679338512253880)
XLA Ops:
  0.0 1.9 %shard_map.46 = (f32[20,4,8,128]{3,2,1,0:T(8,128)S(1)}, f32[25,4,128]{2,1,0:T(4,128)S(1)}, f32[25,4,128]{2,1,0:T(4,128)S(1)}, f32[20,128]{1,0:T(8,128)S(1)}, f32...) custom-call(f32[20,10,8,128]{3,2,1,0:T(8,128)} %bitcast.7, ...), custom_call_target="tpu_custom_call" | custom-call | flops 4915200 | bytes 1228800 | tf_op jit(solution)/shard_map/pallas_call | solution.py:426
  1.9 2.5 %collective-permute-start = (f32[25,4,128]{2,1,0:T(4,128)S(1)}, f32[25,4,128]{2,1,0:T(4,128)S(1)}, u32[]{:S(2)}, u32[]{:S(2)}) collective-permute-start(f32[25,4,128]{2,1,0:T(4,128)S(1)} %get-tuple-element.41), channel_id=1, source_target_pairs={{0,3},{1,2},{2,1},{3,0},{4,7},{5,6},{6,5},{7,4},{8,11},{9,10},{10,... | collective-permute-start | bytes 153608 | tf_op jit(solution)/shard_map/ppermute | solution.py:419
  4.4 0.7 %collective-permute-start.1 = (f32[25,4,128]{2,1,0:T(4,128)S(1)}, f32[25,4,128]{2,1,0:T(4,128)S(1)}, u32[]{:S(2)}, u32[]{:S(2)}) collective-permute-start(f32[25,4,128]{2,1,0:T(4,128)S(1)} %get-tuple-element.42), channel_id=1, source_target_pairs={{0,1},{1,0},{2,3},{3,2},{4,5},{5,4},{6,7},{7,6},{8,9},{9,8},{10,11... | collective-permute-start | bytes 153608 | tf_op jit(solution)/shard_map/ppermute | solution.py:420
  5.1 1.3 %shard_map.47 = (f32[20,10,8,128]{3,2,1,0:T(8,128)S(1)}, f32[10,8,128]{2,1,0:T(8,128)S(1)}, f32[10,8,128]{2,1,0:T(8,128)S(1)}) custom-call(f32[20,10,8,128]{3,2,1,0:T(8,128)S(1)} %get-tuple-element.33.u_ref, f32[20,4,8,128]{3,2,1,0:T(8,128)S(1)} %get-tuple-element.34.edge_ref, f32[20,128]{1,0:T(8,128)S(1)} %get-tuple-element.35.s0, ...), custom_call_target="tpu_custom_call" | custom-call | flops 7372800 | bytes 1843200 | tf_op jit(solution)/shard_map/pallas_call | solution.py:426
  6.4 0.2 collective-permute-done.rb
  6.6 0.0 collective-permute-done.1.ra
  6.6 0.1 shard_map.48
  6.7 5.6 %collective-permute-start.2 = (f32[11,8,128]{2,1,0:T(8,128)S(1)}, f32[11,8,128]{2,1,0:T(8,128)S(1)}, u32[]{:S(2)}, u32[]{:S(2)}) collective-permute-start(f32[11,8,128]{2,1,0:T(8,128)S(1)} %get-tuple-element.48.fb), channel_id=1, source_target_pairs={{0,28},{4,8},{8,4},{12,16},{16,12},{20,24},{24,20},{28,0},{1,29},{... | collective-permute-start | bytes 135176 | tf_op jit(solution)/shard_map/ppermute | solution.py:419
  12.3 0.0 collective-permute-start.3
  12.3 1.3 %shard_map.49 = (f32[12,10,8,128]{3,2,1,0:T(8,128)S(1)}, f32[20,128]{1,0:T(8,128)S(1)}) custom-call(f32[20,10,8,128]{3,2,1,0:T(8,128)S(1)} %get-tuple-element.38.a_ref, f32[20,8,128]{2,1,0:T(8,128)S(1)} %get-tuple-element.44.low_ref, f32[20,8,128]{2,1,0:T(8,128)S(1)} %get-tuple-element.45.high_ref, f32[20,128]{1,0:T(8,128)S(1)} %get-tuple-element.46.mcol_ref, ...), custom_call_target="tpu_custom_call" | custom-call | flops 7372800 | bytes 1843200 | tf_op jit(solution)/shard_map/pallas_call | solution.py:426
  13.6 0.7 %collective-permute-done.2.rb = f32[11,8,128]{2,1,0:T(8,128)S(1)} collective-permute-done((f32[11,8,128]{2,1,0:T(8,128)S(1)}, f32[11,8,128]{2,1,0:T(8,128)S(1)}, u32[]{:S(2)}, u32[]{:S(2)}) %collective-permute-start.2) | collective-permute-done | bytes 45088 | tf_op jit(solution)/shard_map/ppermute | solution.py:419
  14.3 2.0 %collective-permute-done.3.ra = f32[11,8,128]{2,1,0:T(8,128)S(1)} collective-permute-done((f32[11,8,128]{2,1,0:T(8,128)S(1)}, f32[11,8,128]{2,1,0:T(8,128)S(1)}, u32[]{:S(2)}, u32[]{:S(2)}) %collective-permute-start.3) | collective-permute-done | bytes 45088 | tf_op jit(solution)/shard_map/ppermute | solution.py:420
  16.3 1.0 %shard_map.50 = (f32[20,10,8,128]{3,2,1,0:T(8,128)S(1)}, f32[10,8,128]{2,1,0:T(8,128)S(1)}, f32[10,8,128]{2,1,0:T(8,128)S(1)}, f32[20,4,128]{2,1,0:T(4,128)S(1)}...) custom-call(f32[20,10,8,128]{3,2,1,0:T(8,128)S(1)} %get-tuple-element.38.a_ref, ...), custom_call_target="tpu_custom_call" | custom-call | flops 4915200 | bytes 1228800 | tf_op jit(solution)/shard_map/pallas_call | solution.py:426
  17.3 0.1 collective-permute-start.4
  17.4 1.6 %collective-permute-start.5 = (f32[20,4,128]{2,1,0:T(4,128)S(1)}, f32[20,4,128]{2,1,0:T(4,128)S(1)}, u32[]{:S(2)}, u32[]{:S(2)}) collective-permute-start(f32[20,4,128]{2,1,0:T(4,128)S(1)} %get-tuple-element.55), channel_id=1, source_target_pairs={{0,1},{1,0},{2,3},{3,2},{4,5},{5,4},{6,7},{7,6},{8,9},{9,8},{10,11... | collective-permute-start | bytes 122888 | tf_op jit(solution)/shard_map/ppermute | solution.py:420
  19.0 2.1 %collective-permute-done.4.rb = f32[20,4,128]{2,1,0:T(4,128)S(1)} collective-permute-done((f32[20,4,128]{2,1,0:T(4,128)S(1)}, f32[20,4,128]{2,1,0:T(4,128)S(1)}, u32[]{:S(2)}, u32[]{:S(2)}) %collective-permute-start.4) | collective-permute-done | bytes 40992 | tf_op jit(solution)/shard_map/ppermute | solution.py:419
  21.2 0.0 collective-permute-done.5.ra
  21.2 2.8 %collective-permute-start.6 = (f32[10,8,128]{2,1,0:T(8,128)S(1)}, f32[10,8,128]{2,1,0:T(8,128)S(1)}, u32[]{:S(2)}, u32[]{:S(2)}) collective-permute-start(f32[10,8,128]{2,1,0:T(8,128)S(1)} %get-tuple-element.59.fb), channel_id=1, source_target_pairs={{0,28},{4,8},{8,4},{12,16},{16,12},{20,24},{24,20},{28,0},{1,29},{... | collective-permute-start | bytes 122888 | tf_op jit(solution)/shard_map/ppermute | solution.py:419
  24.0 0.0 collective-permute-start.7
  24.0 1.3 %shard_map.52.held = f32[20,10,8,128]{3,2,1,0:T(8,128)} custom-call(f32[20,10,8,128]{3,2,1,0:T(8,128)S(1)} %get-tuple-element.51.a_ref, f32[20,8,128]{2,1,0:T(8,128)S(1)} %get-tuple-element.56.low_ref, f32[20,8,128]{2,1,0:T(8,128)S(1)} %get-tuple-element.57.high_ref, f32[20,128]{1,0:T(8,128)S(1)} %get-tuple-element.58.inv_ref), custom_call_target="tpu_custom_call" | custom-call | flops 2457600 | bytes 614400 | tf_op jit(solution)/shard_map/pallas_call | solution.py:426
  25.2 2.7 %collective-permute-done.6.rb = f32[10,8,128]{2,1,0:T(8,128)S(1)} collective-permute-done((f32[10,8,128]{2,1,0:T(8,128)S(1)}, f32[10,8,128]{2,1,0:T(8,128)S(1)}, u32[]{:S(2)}, u32[]{:S(2)}) %collective-permute-start.6) | collective-permute-done | bytes 40992 | tf_op jit(solution)/shard_map/ppermute | solution.py:419
  28.0 0.4 %collective-permute-done.7.ra = f32[10,8,128]{2,1,0:T(8,128)S(1)} collective-permute-done((f32[10,8,128]{2,1,0:T(8,128)S(1)}, f32[10,8,128]{2,1,0:T(8,128)S(1)}, u32[]{:S(2)}, u32[]{:S(2)}) %collective-permute-start.7) | collective-permute-done | bytes 40992 | tf_op jit(solution)/shard_map/ppermute | solution.py:420
  28.4 0.8 %shard_map.53 = f32[20,10,8,128]{3,2,1,0:T(8,128)} custom-call(f32[20,10,8,128]{3,2,1,0:T(8,128)} %shard_map.52.held, f32[10,8,128]{2,1,0:T(8,128)S(1)} %get-tuple-element.59.fb, f32[10,8,128]{2,1,0:T(8,128)S(1)} %get-tuple-element.60.fa, f32[10,8,128]{2,1,0:T(8,128)S(1)} %collective-permute-done.6.rb, ...), custom_call_target="tpu_custom_call", output_to_operand_aliasing={{}: (0, {})} | custom-call | flops 245760 | bytes 61440 | tf_op jit(solution)/shard_map/pallas_call | solution.py:426
  (1 shorter events, 0.0 us)
Async XLA Ops:
  1.9 4.6 %collective-permute-start = (f32[25,4,128]{2,1,0:T(4,128)S(1)}, f32[25,4,128]{2,1,0:T(4,128)S(1)}, u32[]{:S(2)}, u32[]{:S(2)}) collective-permute-start(f32[25,4,128]{2,1,0:T(4,128)S(1)} %get-tuple-element.41), channel_id=1, source_target_pairs={{0,3},{1,2},{2,1},{3,0},{4,7},{5,6},{6,5},{7,4},{8,11},{9,10},{10,... | collective-permute-start | bytes 153608 | tf_op jit(solution)/shard_map/ppermute | solution.py:419
  4.4 2.2 %collective-permute-start.1 = (f32[25,4,128]{2,1,0:T(4,128)S(1)}, f32[25,4,128]{2,1,0:T(4,128)S(1)}, u32[]{:S(2)}, u32[]{:S(2)}) collective-permute-start(f32[25,4,128]{2,1,0:T(4,128)S(1)} %get-tuple-element.42), channel_id=1, source_target_pairs={{0,1},{1,0},{2,3},{3,2},{4,5},{5,4},{6,7},{7,6},{8,9},{9,8},{10,11... | collective-permute-start | bytes 153608 | tf_op jit(solution)/shard_map/ppermute | solution.py:420
  6.7 7.6 %collective-permute-start.2 = (f32[11,8,128]{2,1,0:T(8,128)S(1)}, f32[11,8,128]{2,1,0:T(8,128)S(1)}, u32[]{:S(2)}, u32[]{:S(2)}) collective-permute-start(f32[11,8,128]{2,1,0:T(8,128)S(1)} %get-tuple-element.48.fb), channel_id=1, source_target_pairs={{0,28},{4,8},{8,4},{12,16},{16,12},{20,24},{24,20},{28,0},{1,29},{... | collective-permute-start | bytes 135176 | tf_op jit(solution)/shard_map/ppermute | solution.py:419
  12.3 4.0 %collective-permute-start.3 = (f32[11,8,128]{2,1,0:T(8,128)S(1)}, f32[11,8,128]{2,1,0:T(8,128)S(1)}, u32[]{:S(2)}, u32[]{:S(2)}) collective-permute-start(f32[11,8,128]{2,1,0:T(8,128)S(1)} %get-tuple-element.49.fa), channel_id=1, source_target_pairs={{0,4},{4,0},{8,12},{12,8},{16,20},{20,16},{24,28},{28,24},{1,5},{5... | collective-permute-start | bytes 135176 | tf_op jit(solution)/shard_map/ppermute | solution.py:420
  17.3 3.8 %collective-permute-start.4 = (f32[20,4,128]{2,1,0:T(4,128)S(1)}, f32[20,4,128]{2,1,0:T(4,128)S(1)}, u32[]{:S(2)}, u32[]{:S(2)}) collective-permute-start(f32[20,4,128]{2,1,0:T(4,128)S(1)} %get-tuple-element.54), channel_id=1, source_target_pairs={{0,3},{1,2},{2,1},{3,0},{4,7},{5,6},{6,5},{7,4},{8,11},{9,10},{10,... | collective-permute-start | bytes 122888 | tf_op jit(solution)/shard_map/ppermute | solution.py:419
  17.4 3.8 %collective-permute-start.5 = (f32[20,4,128]{2,1,0:T(4,128)S(1)}, f32[20,4,128]{2,1,0:T(4,128)S(1)}, u32[]{:S(2)}, u32[]{:S(2)}) collective-permute-start(f32[20,4,128]{2,1,0:T(4,128)S(1)} %get-tuple-element.55), channel_id=1, source_target_pairs={{0,1},{1,0},{2,3},{3,2},{4,5},{5,4},{6,7},{7,6},{8,9},{9,8},{10,11... | collective-permute-start | bytes 122888 | tf_op jit(solution)/shard_map/ppermute | solution.py:420
  21.2 6.8 %collective-permute-start.6 = (f32[10,8,128]{2,1,0:T(8,128)S(1)}, f32[10,8,128]{2,1,0:T(8,128)S(1)}, u32[]{:S(2)}, u32[]{:S(2)}) collective-permute-start(f32[10,8,128]{2,1,0:T(8,128)S(1)} %get-tuple-element.59.fb), channel_id=1, source_target_pairs={{0,28},{4,8},{8,4},{12,16},{16,12},{20,24},{24,20},{28,0},{1,29},{... | collective-permute-start | bytes 122888 | tf_op jit(solution)/shard_map/ppermute | solution.py:419
  24.0 4.4 %collective-permute-start.7 = (f32[10,8,128]{2,1,0:T(8,128)S(1)}, f32[10,8,128]{2,1,0:T(8,128)S(1)}, u32[]{:S(2)}, u32[]{:S(2)}) collective-permute-start(f32[10,8,128]{2,1,0:T(8,128)S(1)} %get-tuple-element.60.fa), channel_id=1, source_target_pairs={{0,4},{4,0},{8,12},{12,8},{16,20},{20,16},{24,28},{28,24},{1,5},{5... | collective-permute-start | bytes 122888 | tf_op jit(solution)/shard_map/ppermute | solution.py:420

commit v4 on v3

--- a/solution.py
+++ b/solution.py
@@ -141,16 +141,20 @@
     u_hbm, md_hbm, mc_hbm, mass_hbm,
     edge_ref, ca_ref, cb_ref, s0, s1, sx, sm, u_ref, md_v, mc_v, mass_v, sem,
 ):
-    rows, pairs = u_ref.shape[:2]
+    rows, pairs = u_hbm.shape[:2]
     cols = 2 * pairs
     bands = rows // 4
 
-    def chunk(e):
+    def chunk(e, k):
         part = pl.ds(4 * e, 4)
-        return pltpu.make_async_copy(u_hbm.at[part], u_ref.at[part], sem.at[e])
+        return pltpu.make_async_copy(
+            u_hbm.at[part, pl.ds((pairs - 2) * k, 2)],
+            u_ref.at[part, pl.ds(2 * k, 2)],
+            sem.at[bands * k + e],
+        )
 
     small = [
-        pltpu.make_async_copy(source, dest, sem.at[bands + k])
+        pltpu.make_async_copy(source, dest, sem.at[2 * bands + k])
         for k, (source, dest) in enumerate(
             ((md_hbm, md_v), (mc_hbm, mc_v), (mass_hbm, mass_v))
         )
@@ -158,7 +162,8 @@
     for copy in small:
         copy.start()
     for e in range(bands):
-        chunk(e).start()
+        chunk(e, 0).start()
+        chunk(e, 1).start()
     for copy in small:
         copy.wait()
     s0[:, 0:cols] = md_v[:, 0, :]
@@ -169,10 +174,11 @@
     upper, fwd, bwd = constants()
 
     def band(e, carry):
-        chunk(e).wait()
+        chunk(e, 0).wait()
+        chunk(e, 1).wait()
         for k, g in enumerate((0, pairs // 2 - 1)):
             done = element(
-                lambda row, a, p: u_ref[row, p], 4 * e, g, (s0, s1, sx), upper, fwd, bwd
+                lambda row, a, p: u_ref[row, p - 2 * g + 2 * k], 4 * e, g, (s0, s1, sx), upper, fwd, bwd
             )
             for a in range(4):
                 for h in range(2):
@@ -195,20 +201,30 @@
         cb_ref[rows + q] = part
 
 
-def first_middle(u_ref, edge_ref, s0, s1, sx, out_ref, rowf_ref, rowl_ref):
-    rows, pairs = u_ref.shape[:2]
+def first_middle(u_hbm, edge_ref, s0, s1, sx, out_ref, rowf_ref, rowl_ref, u_ref, sem):
+    rows, pairs = u_hbm.shape[:2]
+
+    def chunk(e):
+        part = pl.ds(4 * e, 4)
+        return pltpu.make_async_copy(
+            u_hbm.at[part, pl.ds(2, pairs - 4)], u_ref.at[part], sem.at[e]
+        )
+
+    for e in range(rows // 4):
+        chunk(e).start()
     last = pairs // 2 - 1
     upper, fwd, bwd = constants()
 
     def band(e, carry):
         base = 4 * e
+        chunk(e).wait()
 
         def made(g):
             if g in (0, last):
                 k = 0 if g == 0 else 2
                 return [[edge_ref[base + a, k + h] for h in range(2)] for a in range(4)]
             return element(
-                lambda row, a, p: u_ref[row, p], base, g, (s0, s1, sx), upper, fwd, bwd
+                lambda row, a, p: u_ref[row, p - 2], base, g, (s0, s1, sx), upper, fwd, bwd
             )
 
         def put(row, p, v):
@@ -448,18 +464,23 @@
     tall = ((rows + 7) // 8 * 8, 128)
     flops = 60 * rows * pairs * 8 * 128
 
-    ends, ca, cb, s0, s1, sx, sm, uv = call(
+    u, *rest = (
+        pltpu.with_memory_space_constraint(x, pltpu.HBM)
+        for x in (u, md, metric_cross, point_mass)
+    )
+    ends, ca, cb, s0, s1, sx, sm = call(
         first_edges,
-        [(rows, 4, 8, 128)] + [(rows + bands, 4, 128)] * 2 + [line] * 4 + [full],
+        [(rows, 4, 8, 128)] + [(rows + bands, 4, 128)] * 2 + [line] * 4,
         flops * 2 // 5,
-        [pltpu.with_memory_space_constraint(x, pltpu.HBM)
-         for x in (u, md, metric_cross, point_mass)],
-        [VMEM(md.shape, F32), VMEM((rows, cols), F32), VMEM((rows, cols), F32),
-         pltpu.SemaphoreType.DMA((bands + 3,))],
+        [u, *rest],
+        [VMEM((rows, 4, 8, 128), F32), VMEM(md.shape, F32), VMEM((rows, cols), F32), VMEM((rows, cols), F32),
+         pltpu.SemaphoreType.DMA((2 * bands + 3,))],
         far_in=4,
     )
     ga, gb = exchange(ca, cb, "col")
-    a1, rf, rl = call(first_middle, [full, edge, edge], flops * 3 // 5, [uv, ends, s0, s1, sx])
+    a1, rf, rl = call(first_middle, [full, edge, edge], flops * 3 // 5, [u, ends, s0, s1, sx],
+        [VMEM((rows, pairs - 4, 8, 128), F32), pltpu.SemaphoreType.DMA((bands,))], far_in=1,
+    )
     fb, fa, low, high, mcol = call(
         row_slots_mass, [heavy, heavy, side, side, line], flops // 50,
         [rf, rl, gb, ga, sm], [VMEM(tall, F32)] * 3,

time: 29.3 us -> 29.3 us (level)
  Pallas kernels: 7.68 us -> 8.53 us
  starting transfers between devices: 13.2 us -> 12.4 us
    pallas_call x8, Pallas kernels: 7.68 us -> 8.53 us  [call(): pl.pallas_call(kernel, out_shape=[jax.ShapeDtypeStruct(s, F32) for s in o...]
    ppermute x4, starting transfers between devices: 10.9 us -> 10.1 us  [exchange(): got_b = lax.ppermute(slot_b, axis, pairs_b)]
  transfers between devices with their start and end apart: 8 -> 8, of which waited for: 6 -> 5; matrix products, arithmetic and copies ran while one was open for 0% -> 0% of each run, Pallas kernels for 13% -> 16%
where the time goes in v4:
time: 29.3 us; the launch traced here: 29.1 us
  starting transfers between devices  12.4 us (42%)
  Pallas kernels  8.53 us (29%)
  waiting for transfers between devices  8.02 us (27%)
    ppermute x4, starting transfers between devices, exchange(): got_b = lax.ppermute(slot_b, axis, pairs_b)  10.1 us
    pallas_call x8, Pallas kernels, call(): pl.pallas_call(kernel, out_shape=[jax.ShapeDtypeStruct(s, F32) for s in o...  8.53 us
    ppermute x4, waiting for transfers between devices, exchange(): got_b = lax.ppermute(slot_b, axis, pairs_b)  5.55 us
    ppermute x4, waiting for transfers between devices, exchange(): got_a = lax.ppermute(slot_a, axis, pairs_a)  2.46 us
    ppermute x4, starting transfers between devices, exchange(): got_a = lax.ppermute(slot_a, axis, pairs_a)  2.31 us
  transfers between devices with their start and end apart: 8, of which 5 were waited for; matrix products, arithmetic and copies ran while one was open for 0% of the time, Pallas kernels for 16%

profile of v4, /device:TPU:0, one launch (start us, length us, event | category | flops | bytes accessed | tf_op | source)
XLA Modules:
  0.0 29.1 jit_solution(11523415110182960374)
XLA Ops:
  0.0 1.8 %shard_map.46 = (f32[20,4,8,128]{3,2,1,0:T(8,128)S(1)}, f32[25,4,128]{2,1,0:T(4,128)S(1)}, f32[25,4,128]{2,1,0:T(4,128)S(1)}, f32[20,128]{1,0:T(8,128)S(1)}, f32...) custom-call(f32[20,10,8,128]{3,2,1,0:T(8,128)} %bitcast.7, f32[20,2,20]{2,1,0:T(2,128)} %bitcast.9, ...), custom_call_target="tpu_custom_call" | custom-call | flops 4915200 | bytes 1228800 | tf_op jit(solution)/shard_map/pallas_call | solution.py:442
  1.9 2.5 %collective-permute-start = (f32[25,4,128]{2,1,0:T(4,128)S(1)}, f32[25,4,128]{2,1,0:T(4,128)S(1)}, u32[]{:S(2)}, u32[]{:S(2)}) collective-permute-start(f32[25,4,128]{2,1,0:T(4,128)S(1)} %get-tuple-element.39), channel_id=1, source_target_pairs={{0,3},{1,2},{2,1},{3,0},{4,7},{5,6},{6,5},{7,4},{8,11},{9,10},{10,... | collective-permute-start | bytes 153608 | tf_op jit(solution)/shard_map/ppermute | solution.py:435
  4.3 0.7 %collective-permute-start.1 = (f32[25,4,128]{2,1,0:T(4,128)S(1)}, f32[25,4,128]{2,1,0:T(4,128)S(1)}, u32[]{:S(2)}, u32[]{:S(2)}) collective-permute-start(f32[25,4,128]{2,1,0:T(4,128)S(1)} %get-tuple-element.40), channel_id=1, source_target_pairs={{0,1},{1,0},{2,3},{3,2},{4,5},{5,4},{6,7},{7,6},{8,9},{9,8},{10,11... | collective-permute-start | bytes 153608 | tf_op jit(solution)/shard_map/ppermute | solution.py:436
  5.0 2.2 %shard_map.47 = (f32[20,10,8,128]{3,2,1,0:T(8,128)S(1)}, f32[10,8,128]{2,1,0:T(8,128)S(1)}, f32[10,8,128]{2,1,0:T(8,128)S(1)}) custom-call(f32[20,10,8,128]{3,2,1,0:T(8,128)} %bitcast.8, f32[20,4,8,128]{3,2,1,0:T(8,128)S(1)} %get-tuple-element.32.edge_ref, f32[20,128]{1,0:T(8,128)S(1)} %get-tuple-element.33.s0, f32[20,128]{1,0:T(8,128)S(1)} %get-tuple-element.34.s1, ...), custom_call_target="tpu_custom_call" | custom-call | flops 7372800 | bytes 1843200 | tf_op jit(solution)/shard_map/pallas_call | solution.py:442
  7.2 0.0 collective-permute-done.rb
  7.2 0.0 collective-permute-done.1.ra
  7.2 0.1 shard_map.48
  7.3 4.8 %collective-permute-start.2 = (f32[11,8,128]{2,1,0:T(8,128)S(1)}, f32[11,8,128]{2,1,0:T(8,128)S(1)}, u32[]{:S(2)}, u32[]{:S(2)}) collective-permute-start(f32[11,8,128]{2,1,0:T(8,128)S(1)} %get-tuple-element.46.fb), channel_id=1, source_target_pairs={{0,28},{4,8},{8,4},{12,16},{16,12},{20,24},{24,20},{28,0},{1,29},{... | collective-permute-start | bytes 135176 | tf_op jit(solution)/shard_map/ppermute | solution.py:435
  12.2 0.0 collective-permute-start.3
  12.2 1.3 %shard_map.49 = (f32[12,10,8,128]{3,2,1,0:T(8,128)S(1)}, f32[20,128]{1,0:T(8,128)S(1)}) custom-call(f32[20,10,8,128]{3,2,1,0:T(8,128)S(1)} %get-tuple-element.36.a_ref, f32[20,8,128]{2,1,0:T(8,128)S(1)} %get-tuple-element.42.low_ref, f32[20,8,128]{2,1,0:T(8,128)S(1)} %get-tuple-element.43.high_ref, f32[20,128]{1,0:T(8,128)S(1)} %get-tuple-element.44.mcol_ref, ...), custom_call_target="tpu_custom_call" | custom-call | flops 7372800 | bytes 1843200 | tf_op jit(solution)/shard_map/pallas_call | solution.py:442
  13.5 0.7 %collective-permute-done.2.rb = f32[11,8,128]{2,1,0:T(8,128)S(1)} collective-permute-done((f32[11,8,128]{2,1,0:T(8,128)S(1)}, f32[11,8,128]{2,1,0:T(8,128)S(1)}, u32[]{:S(2)}, u32[]{:S(2)}) %collective-permute-start.2) | collective-permute-done | bytes 45088 | tf_op jit(solution)/shard_map/ppermute | solution.py:435
  14.2 2.0 %collective-permute-done.3.ra = f32[11,8,128]{2,1,0:T(8,128)S(1)} collective-permute-done((f32[11,8,128]{2,1,0:T(8,128)S(1)}, f32[11,8,128]{2,1,0:T(8,128)S(1)}, u32[]{:S(2)}, u32[]{:S(2)}) %collective-permute-start.3) | collective-permute-done | bytes 45088 | tf_op jit(solution)/shard_map/ppermute | solution.py:436
  16.2 1.0 %shard_map.50 = (f32[20,10,8,128]{3,2,1,0:T(8,128)S(1)}, f32[10,8,128]{2,1,0:T(8,128)S(1)}, f32[10,8,128]{2,1,0:T(8,128)S(1)}, f32[20,4,128]{2,1,0:T(4,128)S(1)}...) custom-call(f32[20,10,8,128]{3,2,1,0:T(8,128)S(1)} %get-tuple-element.36.a_ref, ...), custom_call_target="tpu_custom_call" | custom-call | flops 4915200 | bytes 1228800 | tf_op jit(solution)/shard_map/pallas_call | solution.py:442
  17.2 0.1 collective-permute-start.4
  17.3 1.6 %collective-permute-start.5 = (f32[20,4,128]{2,1,0:T(4,128)S(1)}, f32[20,4,128]{2,1,0:T(4,128)S(1)}, u32[]{:S(2)}, u32[]{:S(2)}) collective-permute-start(f32[20,4,128]{2,1,0:T(4,128)S(1)} %get-tuple-element.53), channel_id=1, source_target_pairs={{0,1},{1,0},{2,3},{3,2},{4,5},{5,4},{6,7},{7,6},{8,9},{9,8},{10,11... | collective-permute-start | bytes 122888 | tf_op jit(solution)/shard_map/ppermute | solution.py:436
  18.9 2.1 %collective-permute-done.4.rb = f32[20,4,128]{2,1,0:T(4,128)S(1)} collective-permute-done((f32[20,4,128]{2,1,0:T(4,128)S(1)}, f32[20,4,128]{2,1,0:T(4,128)S(1)}, u32[]{:S(2)}, u32[]{:S(2)}) %collective-permute-start.4) | collective-permute-done | bytes 40992 | tf_op jit(solution)/shard_map/ppermute | solution.py:435
  21.1 0.0 collective-permute-done.5.ra
  21.1 2.8 %collective-permute-start.6 = (f32[10,8,128]{2,1,0:T(8,128)S(1)}, f32[10,8,128]{2,1,0:T(8,128)S(1)}, u32[]{:S(2)}, u32[]{:S(2)}) collective-permute-start(f32[10,8,128]{2,1,0:T(8,128)S(1)} %get-tuple-element.57.fb), channel_id=1, source_target_pairs={{0,28},{4,8},{8,4},{12,16},{16,12},{20,24},{24,20},{28,0},{1,29},{... | collective-permute-start | bytes 122888 | tf_op jit(solution)/shard_map/ppermute | solution.py:435
  23.9 0.0 collective-permute-start.7
  23.9 1.3 %shard_map.52.held = f32[20,10,8,128]{3,2,1,0:T(8,128)} custom-call(f32[20,10,8,128]{3,2,1,0:T(8,128)S(1)} %get-tuple-element.49.a_ref, f32[20,8,128]{2,1,0:T(8,128)S(1)} %get-tuple-element.54.low_ref, f32[20,8,128]{2,1,0:T(8,128)S(1)} %get-tuple-element.55.high_ref, f32[20,128]{1,0:T(8,128)S(1)} %get-tuple-element.56.inv_ref), custom_call_target="tpu_custom_call" | custom-call | flops 2457600 | bytes 614400 | tf_op jit(solution)/shard_map/pallas_call | solution.py:442
  25.1 2.7 %collective-permute-done.6.rb = f32[10,8,128]{2,1,0:T(8,128)S(1)} collective-permute-done((f32[10,8,128]{2,1,0:T(8,128)S(1)}, f32[10,8,128]{2,1,0:T(8,128)S(1)}, u32[]{:S(2)}, u32[]{:S(2)}) %collective-permute-start.6) | collective-permute-done | bytes 40992 | tf_op jit(solution)/shard_map/ppermute | solution.py:435
  27.9 0.4 %collective-permute-done.7.ra = f32[10,8,128]{2,1,0:T(8,128)S(1)} collective-permute-done((f32[10,8,128]{2,1,0:T(8,128)S(1)}, f32[10,8,128]{2,1,0:T(8,128)S(1)}, u32[]{:S(2)}, u32[]{:S(2)}) %collective-permute-start.7) | collective-permute-done | bytes 40992 | tf_op jit(solution)/shard_map/ppermute | solution.py:436
  28.3 0.8 %shard_map.53 = f32[20,10,8,128]{3,2,1,0:T(8,128)} custom-call(f32[20,10,8,128]{3,2,1,0:T(8,128)} %shard_map.52.held, f32[10,8,128]{2,1,0:T(8,128)S(1)} %get-tuple-element.57.fb, f32[10,8,128]{2,1,0:T(8,128)S(1)} %get-tuple-element.58.fa, f32[10,8,128]{2,1,0:T(8,128)S(1)} %collective-permute-done.6.rb, ...), custom_call_target="tpu_custom_call", output_to_operand_aliasing={{}: (0, {})} | custom-call | flops 245760 | bytes 61440 | tf_op jit(solution)/shard_map/pallas_call | solution.py:442
  (1 shorter events, 0.0 us)
Async XLA Ops:
  1.9 5.4 %collective-permute-start = (f32[25,4,128]{2,1,0:T(4,128)S(1)}, f32[25,4,128]{2,1,0:T(4,128)S(1)}, u32[]{:S(2)}, u32[]{:S(2)}) collective-permute-start(f32[25,4,128]{2,1,0:T(4,128)S(1)} %get-tuple-element.39), channel_id=1, source_target_pairs={{0,3},{1,2},{2,1},{3,0},{4,7},{5,6},{6,5},{7,4},{8,11},{9,10},{10,... | collective-permute-start | bytes 153608 | tf_op jit(solution)/shard_map/ppermute | solution.py:435
  4.3 2.9 %collective-permute-start.1 = (f32[25,4,128]{2,1,0:T(4,128)S(1)}, f32[25,4,128]{2,1,0:T(4,128)S(1)}, u32[]{:S(2)}, u32[]{:S(2)}) collective-permute-start(f32[25,4,128]{2,1,0:T(4,128)S(1)} %get-tuple-element.40), channel_id=1, source_target_pairs={{0,1},{1,0},{2,3},{3,2},{4,5},{5,4},{6,7},{7,6},{8,9},{9,8},{10,11... | collective-permute-start | bytes 153608 | tf_op jit(solution)/shard_map/ppermute | solution.py:436
  7.3 6.8 %collective-permute-start.2 = (f32[11,8,128]{2,1,0:T(8,128)S(1)}, f32[11,8,128]{2,1,0:T(8,128)S(1)}, u32[]{:S(2)}, u32[]{:S(2)}) collective-permute-start(f32[11,8,128]{2,1,0:T(8,128)S(1)} %get-tuple-element.46.fb), channel_id=1, source_target_pairs={{0,28},{4,8},{8,4},{12,16},{16,12},{20,24},{24,20},{28,0},{1,29},{... | collective-permute-start | bytes 135176 | tf_op jit(solution)/shard_map/ppermute | solution.py:435
  12.2 4.0 %collective-permute-start.3 = (f32[11,8,128]{2,1,0:T(8,128)S(1)}, f32[11,8,128]{2,1,0:T(8,128)S(1)}, u32[]{:S(2)}, u32[]{:S(2)}) collective-permute-start(f32[11,8,128]{2,1,0:T(8,128)S(1)} %get-tuple-element.47.fa), channel_id=1, source_target_pairs={{0,4},{4,0},{8,12},{12,8},{16,20},{20,16},{24,28},{28,24},{1,5},{5... | collective-permute-start | bytes 135176 | tf_op jit(solution)/shard_map/ppermute | solution.py:436
  17.2 3.8 %collective-permute-start.4 = (f32[20,4,128]{2,1,0:T(4,128)S(1)}, f32[20,4,128]{2,1,0:T(4,128)S(1)}, u32[]{:S(2)}, u32[]{:S(2)}) collective-permute-start(f32[20,4,128]{2,1,0:T(4,128)S(1)} %get-tuple-element.52), channel_id=1, source_target_pairs={{0,3},{1,2},{2,1},{3,0},{4,7},{5,6},{6,5},{7,4},{8,11},{9,10},{10,... | collective-permute-start | bytes 122888 | tf_op jit(solution)/shard_map/ppermute | solution.py:435
  17.3 3.8 %collective-permute-start.5 = (f32[20,4,128]{2,1,0:T(4,128)S(1)}, f32[20,4,128]{2,1,0:T(4,128)S(1)}, u32[]{:S(2)}, u32[]{:S(2)}) collective-permute-start(f32[20,4,128]{2,1,0:T(4,128)S(1)} %get-tuple-element.53), channel_id=1, source_target_pairs={{0,1},{1,0},{2,3},{3,2},{4,5},{5,4},{6,7},{7,6},{8,9},{9,8},{10,11... | collective-permute-start | bytes 122888 | tf_op jit(solution)/shard_map/ppermute | solution.py:436
  21.1 6.8 %collective-permute-start.6 = (f32[10,8,128]{2,1,0:T(8,128)S(1)}, f32[10,8,128]{2,1,0:T(8,128)S(1)}, u32[]{:S(2)}, u32[]{:S(2)}) collective-permute-start(f32[10,8,128]{2,1,0:T(8,128)S(1)} %get-tuple-element.57.fb), channel_id=1, source_target_pairs={{0,28},{4,8},{8,4},{12,16},{16,12},{20,24},{24,20},{28,0},{1,29},{... | collective-permute-start | bytes 122888 | tf_op jit(solution)/shard_map/ppermute | solution.py:435
  23.9 4.4 %collective-permute-start.7 = (f32[10,8,128]{2,1,0:T(8,128)S(1)}, f32[10,8,128]{2,1,0:T(8,128)S(1)}, u32[]{:S(2)}, u32[]{:S(2)}) collective-permute-start(f32[10,8,128]{2,1,0:T(8,128)S(1)} %get-tuple-element.58.fa), channel_id=1, source_target_pairs={{0,4},{4,0},{8,12},{12,8},{16,20},{20,16},{24,28},{28,24},{1,5},{5... | collective-permute-start | bytes 122888 | tf_op jit(solution)/shard_map/ppermute | solution.py:436
